TPU v7x, 256 devices: a whole 4x4x8 slice. The times are simulated.
256 devices in a mesh: dom: 128 (over x, z, y), field: 2 (over core).
Axes of the slice: x: 4, y: 4, z: 8, core: 2. Of those that a mesh axis runs over, the one named last changes fastest.
Arguments:
- ocean: bfloat16 [30, 262144], P('field', 'dom'), may hold values from -6 to 6
- grad_weight: bfloat16 [2048, 4, 128, 256], P('dom'), may hold values from -0.25 to 0.25
- neighbours: int32 [2048, 4], P('dom'), may hold values from 0 to 2047, as said below
- remap_weight: bfloat16 [16384, 384, 128], P(('dom', 'field')), may hold values from -0.109375 to 0.109375
- tile_src: int32 [16384], P(('dom', 'field')), may hold values from 0 to 2047, as said below
- tile_atm: int32 [16384], P(('dom', 'field')), may hold values from 0 to 2047, as said below
- atm_owner: int32 [2048], replicated, may hold values from 0 to 2047, as said below
Outputs:
- atmosphere: float32 [30, 262144], P('field', 'dom')
Inputs may be any that keep to these rules, and one draw needn't show every extreme that they name: `neighbours`: the stencil of a block of partition p holds blocks of p, the last 2 blocks of partition p - 1 or the first 2 blocks of partition p + 1 (partitions are the aligned runs of 16 blocks; no wrap). `tile_src`: tile t names a block of partition t // 128, the partition that holds the tile. `tile_atm`: of the aligned runs of 64 tiles, no run has more than 2 tiles whose atmosphere tile has owner position in one aligned run of 16; in every draw each run reaches 2 for some owner. `atm_owner`: A permutation of the atmosphere tiles.
All inputs are finite; a program needn't handle non-finite values.
Results may differ from a plain program's by a relative error of at most 0.0042.
Values may be sent and summed in bfloat16 or wider, within the bound.
A program may use at most 64 MiB of HBM per device.

v0:
```python
import jax
import jax.numpy as jnp
from jax import lax
from jax.sharding import PartitionSpec as P


def padded_2(shard, sides, width):
    for axis, dim in sides:
        size, length = (lax.axis_size(axis), shard.shape[dim])
        up = [(i, (i + 1) % size) for i in range(size - 1)]
        down = [(j, i) for i, j in up]
        last = lax.slice_in_dim(shard, length - width, length, axis=dim)
        initial = lax.slice_in_dim(shard, 0, width, axis=dim)
        before = lax.ppermute(last, axis, up)
        after = lax.ppermute(initial, axis, down)
        shard = jnp.concatenate([before, shard, after], axis=dim)
    return shard


def joined_along(parts, dim):
    parts = jnp.moveaxis(parts, 0, dim)
    lengths = parts.shape
    return parts.reshape(*lengths[:dim], lengths[dim] * lengths[dim + 1], *lengths[dim + 2 :])


def copy_for_each(shard, axis):
    length = lax.axis_size(axis)
    return lax.all_to_all(
        jnp.broadcast_to(shard[None], (length, *shard.shape)), axis, 0, 0, tiled=True
    )


def collect(shard, axis, dim):
    return joined_along(copy_for_each(shard, axis), dim)


def cut_along(shard, dim, length):
    lengths = shard.shape
    parts = shard.reshape(*lengths[:dim], length, lengths[dim] // length, *lengths[dim + 1 :])
    return jnp.moveaxis(parts, dim, 0)


def summed_on_arrival(shard, axis, dim):
    parts = cut_along(shard, dim, lax.axis_size(axis))
    arrived = lax.all_to_all(parts, axis, split_axis=0, concat_axis=0, tiled=True)
    return arrived.sum(axis=0)


def deliver(contribution, target_dev, local_slot, devices, capacity, owned):
    tile_count = target_dev.shape[0]
    tile_order = jnp.arange(tile_count, dtype=jnp.int32)
    before = jnp.sum(
        (
            (target_dev[:, None] == target_dev[None, :])
            & (tile_order[None, :] < tile_order[:, None])
        ).astype(jnp.int32),
        axis=1,
    )
    position = target_dev * capacity + before
    slot_count = devices * capacity
    matches = position[None, :] == jnp.arange(slot_count, dtype=jnp.int32)[:, None]
    chosen = jnp.sum(jnp.where(matches, tile_order[None, :], 0), axis=1)
    filled = jnp.any(matches, axis=1)
    outgoing = jnp.where(filled[:, None, None], contribution[chosen], 0.0)
    targets = jnp.where(filled, local_slot[chosen], -1)
    incoming, in_targets = (
        lax.all_to_all(
            outgoing.astype(jnp.bfloat16), "dom", split_axis=0, concat_axis=0, tiled=True
        ).astype(outgoing.dtype),
        lax.all_to_all(targets, "dom", split_axis=0, concat_axis=0, tiled=True),
    )
    selector = (in_targets[None, :] == jnp.arange(owned, dtype=jnp.int32)[:, None]).astype(
        jnp.float32
    )
    summed = jnp.einsum("ak,kfc->fac", selector, incoming, precision=lax.Precision.HIGHEST)
    return summed.reshape(summed.shape[0], owned * summed.shape[2])


def local(ocean, grad_weight, neighbours, remap_weight, tile_src, tile_atm, atm_owner):
    block_len = grad_weight.shape[2]
    field_rows = ocean.shape[0]
    nblocks = grad_weight.shape[0]
    device = lax.axis_index("dom")
    devices = lax.axis_size("dom")
    per_core = tile_atm.shape[0]
    capacity_base = max(2, 4 * per_core // devices)
    padded = padded_2(ocean, (("dom", 1),), nblocks * block_len)
    first_block = device * nblocks - nblocks
    extended = padded.reshape(field_rows, -1, block_len)
    local_ids = neighbours - first_block
    picked = jnp.take(extended, local_ids, axis=1)
    gradient = jnp.einsum(
        "fbkj,bkjo->fbo", picked, grad_weight, preferred_element_type=jnp.float32
    ).astype(jnp.bfloat16)
    source = jnp.concatenate([ocean.reshape(field_rows, nblocks, block_len), gradient], axis=2)
    source = collect(source, "field", 0)
    local_src = tile_src - device * nblocks
    source_rows = jnp.take(source, local_src, axis=1)
    contribution = jnp.einsum(
        "ftj,tjc->tfc", source_rows, remap_weight, preferred_element_type=jnp.float32
    )
    atm_tiles = atm_owner.shape[0]
    atm_slot = jnp.sum(
        jnp.where(
            tile_atm[:, None] == jnp.arange(atm_tiles, dtype=jnp.int32)[None, :],
            atm_owner[None, :],
            0,
        ),
        axis=1,
    )
    owned = atm_tiles // devices
    target_dev = atm_slot // owned
    local_slot = atm_slot % owned
    summed = deliver(contribution, target_dev, local_slot, devices, capacity_base, owned)
    return summed_on_arrival(summed, "field", 0)


def solution(mesh):
    in_specs = (
        P("field", "dom"),
        P("dom", None, None, None),
        P("dom", None),
        P(("dom", "field"), None, None),
        P(("dom", "field")),
        P(("dom", "field")),
        P(),
    )
    out_specs = P("field", "dom")
    return jax.shard_map(local, mesh=mesh, in_specs=in_specs, out_specs=out_specs, check_vma=False)
```

profile of v0, /device:TPU:1, one launch (start us, length us, event | category | flops | bytes accessed | tf_op | source)
XLA Modules:
  0.0 117.9 jit_solution(16398224569645400603)
XLA Ops:
  0.0 4.0 %collective-permute-start = (bf16[15,2048]{1,0:T(8,128)(2,1)}, bf16[15,2048]{1,0:T(8,128)(2,1)S(1)}, u32[]{:S(2)}, u32[]{:S(2)}) collective-permute-start(bf16[15,2048]{1,0:T(8,128)(2,1)} %param.7), channel_id=1, source_target_pairs={{0,2},{2,4},{4,6},{6,8},{8,10},{10,12},{12,14},{14,16},{16,18},{18... | collective-permute-start | bytes 184328 | tf_op jit(solution)/shard_map/ppermute | solution.py:14
  4.0 1.3 %collective-permute-start.1 = (bf16[15,2048]{1,0:T(8,128)(2,1)}, bf16[15,2048]{1,0:T(8,128)(2,1)S(1)}, u32[]{:S(2)}, u32[]{:S(2)}) collective-permute-start(bf16[15,2048]{1,0:T(8,128)(2,1)} %param.7), channel_id=1, source_target_pairs={{2,0},{4,2},{6,4},{8,6},{10,8},{12,10},{14,12},{16,14},{18,16},{20... | collective-permute-start | bytes 184328 | tf_op jit(solution)/shard_map/ppermute | solution.py:15
  5.3 0.9 select_reduce_fusion
  6.3 0.2 convert_reduce_fusion
  6.5 0.1 fusion.16
  6.6 0.1 select_reduce_fusion.1
  6.7 0.7 compare_and_fusion.1
  7.3 0.7 compare_and_fusion
  8.0 0.1 copy.31
  8.2 0.1 copy.32
  8.2 0.1 reshape.104
  8.3 1.9 %gather_fusion.3 = s32[256]{0:T(256)S(1)} fusion(s32[64]{0:T(128)S(1)} %get-tuple-element.9, s32[1024]{0:T(1024)S(1)} %pad_clamp_fusion), kind=kCustom, calls=%fused_computation.3 | custom fusion | bytes 3072 | tf_op jit(solution)/shard_map/gather | solution.py:65
  10.2 0.8 select_n.88
  11.0 0.8 copy.40
  11.9 0.0 collective-permute-done
  11.9 0.0 collective-permute-done.1
  11.9 0.9 pad_maximum_fusion
  12.8 0.1 copy.33
  12.9 0.6 gather_fusion
  13.5 2.9 %fusion.10 = bf16[15,16,256]{2,0,1:T(8,128)(2,1)S(1)} fusion(bf16[16,4,128,256]{3,2,1,0:T(8,128)(2,1)} %param.8, bf16[16,4,15,128]{3,2,1,0:T(8,128)(2,1)S(1)} %bitcast.35, pred[16,4]{1,0:T(8,128)(4,1)S(1)} %copy.31), kind=kOutput, calls=%fused_computation.14 | convolution fusion | flops 63098880 | bytes 4563008 | tf_op jit(solution)/shard_map/fbkj,bkjo->fbo/dot_general | solution.py:92
  16.5 4.6 %all_to_all.21 = bf16[2,15,16,384]{3,2,1,0:T(8,128)(2,1)S(1)} all-to-all(bf16[2,15,16,384]{3,2,1,0:T(8,128)(2,1)S(1)} %broadcast_in_dim.92), channel_id=1, replica_groups=mesh['dom'=128,'field'=2] {'field'}, dimensions={0} | all-to-all | bytes 737280 | tf_op jit(solution)/shard_map/all_to_all | solution.py:28
  21.1 17.3 %all-to-all-start.2 = ((s32[128,2,1]{1,2,0:T(1,128)}), s32[128,2,1]{1,2,0:T(1,128)S(1)}, u32[]{:S(2)}, u32[]{:S(2)}) async-start(s32[128,2,1]{1,2,0:T(1,128)} %bitcast.9), calls=%async_computation.2 | async-start | bytes 131072 | tf_op jit(solution)/shard_map/all_to_all | solution.py:70
  38.4 0.1 copy.36
  38.5 0.9 gather_fusion.1
  39.4 4.0 %fusion.2 = bf16[64,30,128]{2,1,0:T(8,128)(2,1)S(1)} fusion(bf16[64,384,128]{2,1,0:T(8,128)(2,1)} %param.10, bf16[64,30,384]{2,1,0:T(8,128)(2,1)S(1)} %gather_fusion.1, pred[64]{0:T(512)(128)(4,1)S(1)} %get-tuple-element.5), kind=kOutput, calls=%fused_computation.7 | convolution fusion | flops 189480960 | bytes 8257600 | tf_op jit(solution)/shard_map/ftj,tjc->tfc/dot_general | solution.py:99
  43.5 1.0 gather_fusion.2
  44.5 2.0 %select_convert_fusion = bf16[256,30,128]{2,1,0:T(8,128)(2,1)} fusion(bf16[256,30,128]{2,1,0:T(8,128)(2,1)S(1)} %gather_fusion.2, pred[256]{0:T(512)(128)(4,1)S(1)} %fusion.16), kind=kLoop, calls=%fused_computation.4 | loop fusion | flops 983040 | bytes 3932416 | tf_op jit(solution)/shard_map/convert_element_type | solution.py:68
  46.4 2.5 %all-to-all-done.2 = s32[128,2,1]{1,2,0:T(1,128)S(1)} async-done(((s32[128,2,1]{1,2,0:T(1,128)}), s32[128,2,1]{1,2,0:T(1,128)S(1)}, u32[]{:S(2)}, u32[]{:S(2)}) %all-to-all-start.2) | async-done | bytes 1056 | tf_op jit(solution)/shard_map/all_to_all | solution.py:70
  48.9 10.7 %all-to-all-start.1 = ((bf16[256,30,128]{2,1,0:T(8,128)(2,1)}), bf16[256,30,128]{2,1,0:T(8,128)(2,1)S(1)}, u32[]{:S(2)}, u32[]{:S(2)}) async-start(bf16[256,30,128]{2,1,0:T(8,128)(2,1)} %select_convert_fusion), calls=%async_computation.1 | async-start | bytes 4194304 | tf_op jit(solution)/shard_map/all_to_all | solution.py:67
  59.7 0.5 broadcast.181
  60.2 0.8 reduce.3
  61.0 0.1 eq.65
  61.2 47.7 %all-to-all-done.1 = bf16[256,30,128]{2,1,0:T(8,128)(2,1)S(1)} async-done(((bf16[256,30,128]{2,1,0:T(8,128)(2,1)}), bf16[256,30,128]{2,1,0:T(8,128)(2,1)S(1)}, u32[]{:S(2)}, u32[]{:S(2)}) %all-to-all-start.1) | async-done | bytes 1966112 | tf_op jit(solution)/shard_map/all_to_all | solution.py:67
  108.8 0.7 fusion.6
  109.5 7.7 %all_to_all.22 = f32[2,15,2048]{2,1,0:T(8,128)S(1)} all-to-all(f32[2,15,2048]{2,1,0:T(8,128)S(1)} %reshape_reshape.3), channel_id=1, replica_groups=mesh['dom'=128,'field'=2] {'field'}, dimensions={0} | all-to-all | bytes 491520 | tf_op jit(solution)/shard_map/all_to_all | solution.py:45
  117.3 0.7 reduce_sum.42
  (15 shorter events, 0.3 us)
Async XLA Ops:
  0.0 11.9 %collective-permute-start = (bf16[15,2048]{1,0:T(8,128)(2,1)}, bf16[15,2048]{1,0:T(8,128)(2,1)S(1)}, u32[]{:S(2)}, u32[]{:S(2)}) collective-permute-start(bf16[15,2048]{1,0:T(8,128)(2,1)} %param.7), channel_id=1, source_target_pairs={{0,2},{2,4},{4,6},{6,8},{8,10},{10,12},{12,14},{14,16},{16,18},{18... | collective-permute-start | bytes 184328 | tf_op jit(solution)/shard_map/ppermute | solution.py:14
  4.0 7.9 %collective-permute-start.1 = (bf16[15,2048]{1,0:T(8,128)(2,1)}, bf16[15,2048]{1,0:T(8,128)(2,1)S(1)}, u32[]{:S(2)}, u32[]{:S(2)}) collective-permute-start(bf16[15,2048]{1,0:T(8,128)(2,1)} %param.7), channel_id=1, source_target_pairs={{2,0},{4,2},{6,4},{8,6},{10,8},{12,10},{14,12},{16,14},{18,16},{20... | collective-permute-start | bytes 184328 | tf_op jit(solution)/shard_map/ppermute | solution.py:15
  21.1 27.8 %all-to-all-start.2 = ((s32[128,2,1]{1,2,0:T(1,128)}), s32[128,2,1]{1,2,0:T(1,128)S(1)}, u32[]{:S(2)}, u32[]{:S(2)}) async-start(s32[128,2,1]{1,2,0:T(1,128)} %bitcast.9), calls=%async_computation.2 | async-start | bytes 131072 | tf_op jit(solution)/shard_map/all_to_all | solution.py:70
  48.9 59.9 %all-to-all-start.1 = ((bf16[256,30,128]{2,1,0:T(8,128)(2,1)}), bf16[256,30,128]{2,1,0:T(8,128)(2,1)S(1)}, u32[]{:S(2)}, u32[]{:S(2)}) async-start(bf16[256,30,128]{2,1,0:T(8,128)(2,1)} %select_convert_fusion), calls=%async_computation.1 | async-start | bytes 4194304 | tf_op jit(solution)/shard_map/all_to_all | solution.py:67
where the time goes:
time: 119 us; the launch traced here: 118 us
  waiting for transfers between devices  50.2 us (42%)
  starting transfers between devices  33.3 us (28%)
  blocking collectives  12.3 us (10%)
  matrix products  7.59 us (6%)
  local copies, waits for them, and re-layouts  7.24 us (6%)
  other arithmetic  7.06 us (6%)
    all_to_all x1, waiting for transfers between devices, deliver(): lax.all_to_all(outgoing.astype(jnp.bfloat16), 'dom', split_axis=0, concat...  47.7 us
    all_to_all x1, starting transfers between devices, deliver(): lax.all_to_all(targets, 'dom', split_axis=0, concat_axis=0, tiled=True)  17.3 us
    all_to_all x1, starting transfers between devices, deliver(): lax.all_to_all(outgoing.astype(jnp.bfloat16), 'dom', split_axis=0, concat...  10.7 us
    all_to_all x1, blocking collectives, summed_on_arrival(): lax.all_to_all(parts, axis, split_axis=0, concat_axis=0, tiled=True)  7.74 us
    all_to_all x1, blocking collectives, copy_for_each(): lax.all_to_all(jnp.broadcast_to(shard[None], (length, *shard.shape)), axi...  4.6 us
    dot_general x1, matrix products, local(): jnp.einsum('ftj,tjc->tfc', source_rows, remap_weight, preferred_element_t...  4.05 us
    ppermute x1, starting transfers between devices, padded_2(): before = lax.ppermute(last, axis, up)  4.01 us
    dot_general x1, matrix products, local(): jnp.einsum('fbkj,bkjo->fbo', picked, grad_weight, preferred_element_type=...  2.88 us
  transfers between devices with their start and end apart: 4, of which 2 were waited for; matrix products, arithmetic and copies ran while one was open for 14% of the time, Pallas kernels for 0%

commit v1 on v0

v1 whole, which is shorter than its diff:
```python
import functools

import jax
import jax.numpy as jnp
from jax import lax
from jax.experimental import pallas as pl
from jax.experimental.pallas import tpu as pltpu
from jax.sharding import PartitionSpec as P

MESH = pl.DeviceIdType.MESH
NX, NZ, NY = 4, 8, 4
PLANE = NX * NY
HALF = 15
BLK = 128
NB = 16
NH = 2
EXT = NB + 2 * NH
TILES = 64
SLOTS = 16
SRC_ROWS = 16
FCH = 3
CHUNKS = HALF // FCH
PITCH = 40
OPITCH = 24


def coords():
    d = lax.axis_index("dom")
    return lax.div(d, NZ * NY), lax.rem(lax.div(d, NY), NZ), lax.rem(d, NY)


def chip(x, z, y):
    return (x * NZ + z) * NY + y


def kernel(
    ocean_hbm,
    gw_hbm,
    nb_ref,
    rw_hbm,
    src_ref,
    rows_ref,
    meta_ref,
    out_ref,
    raw,
    wide,
    gw,
    rw,
    grads,
    cont,
    fields,
    pack,
    sent,
    sent_meta,
    got,
    got_meta,
    select,
    part,
    own,
    zgot,
    last,
    load_sem,
    w_sem,
    oc_send,
    oc_recv,
    gr_send,
    gr_recv,
    me_send,
    me_recv,
    pl_send,
    pl_recv,
    z_send,
    z_recv,
):
    c = lax.axis_index("field")
    d = lax.axis_index("dom")
    x, z, y = coords()
    other = 1 - c
    devices = NX * NZ * NY
    up, down = lax.rem(d + 1, devices), lax.rem(d + devices - 1, devices)

    def plane_chip(j):
        return chip(lax.rem(x + lax.div(j, NY), NX), z, lax.rem(y + lax.rem(j, NY), NY))

    def line_chip(dz):
        return chip(x, lax.rem(z + dz, NZ), y)

    ocean_in = pltpu.make_async_copy(
        ocean_hbm, raw.at[c, :, pl.ds(NH * BLK, NB * BLK)], load_sem.at[0]
    )
    ocean_in.start()
    gw_in = pltpu.make_async_copy(
        gw_hbm.at[pl.ds(c * (NB // 2), NB // 2)], gw, load_sem.at[1]
    )
    gw_in.start()
    rw_in = pltpu.make_async_copy(rw_hbm, rw, w_sem)
    rw_in.start()

    barrier = pltpu.get_barrier_semaphore()

    def greet(dom, core):
        pl.semaphore_signal(
            barrier, inc=1, device_id={"dom": dom, "field": core}, device_id_type=MESH
        )

    greet(d, other)
    for h in range(2):
        greet(up, h)
        greet(down, h)

    def greet_plane(j, _):
        greet(plane_chip(j), 0)
        greet(plane_chip(j), 1)
        return 0

    lax.fori_loop(1, PLANE, greet_plane, 0)

    def greet_line(dz, _):
        greet(line_chip(dz), c)
        return 0

    lax.fori_loop(1, NZ, greet_line, 0)

    target = rows_ref[...]
    row_of = lax.broadcasted_iota(jnp.int32, (PLANE * SRC_ROWS, TILES), 0)
    pack[...] = jnp.where(row_of == target, 1.0, 0.0).astype(jnp.bfloat16)
    packed_meta = jnp.dot(pack[...], meta_ref[...], preferred_element_type=jnp.float32)
    sent_meta[...] = packed_meta.astype(jnp.bfloat16)
    ocean_in.wait()

    pl.semaphore_wait(barrier, 1 + 4 + 2 * (PLANE - 1) + (NZ - 1))

    def remote(src, dst, send, recv, dom, core):
        return pltpu.make_async_remote_copy(
            src_ref=src,
            dst_ref=dst,
            send_sem=send,
            recv_sem=recv,
            device_id={"dom": dom, "field": core},
            device_id_type=MESH,
        )

    first = pl.ds(NH * BLK, NH * BLK)
    final = pl.ds(NB * BLK, NH * BLK)
    left = pl.ds(0, NH * BLK)
    right = pl.ds((NB + NH) * BLK, NH * BLK)
    middle = pl.ds(NH * BLK, NB * BLK)
    ocean_copies = [
        remote(raw.at[c, :, final], raw.at[c, :, left], oc_send.at[0], oc_recv.at[0], up, c),
        remote(raw.at[c, :, final], raw.at[c, :, left], oc_send.at[1], oc_recv.at[1], up, other),
        remote(raw.at[c, :, first], raw.at[c, :, right], oc_send.at[2], oc_recv.at[2], down, c),
        remote(raw.at[c, :, first], raw.at[c, :, right], oc_send.at[3], oc_recv.at[3], down, other),
        remote(raw.at[c, :, middle], raw.at[c, :, middle], oc_send.at[4], oc_recv.at[4], d, other),
    ]
    for copy in ocean_copies:
        copy.start()

    meta_partner = remote(
        sent_meta.at[pl.ds(15 * SRC_ROWS, SRC_ROWS)],
        got_meta.at[pl.ds(30 * SRC_ROWS, SRC_ROWS)],
        me_send,
        me_recv,
        d,
        other,
    )
    meta_partner.start()

    def send_meta(j, _):
        dom = plane_chip(j)
        for h in range(2):
            remote(
                sent_meta.at[pl.ds(pl.multiple_of((j - 1) * SRC_ROWS, SRC_ROWS), SRC_ROWS)],
                got_meta.at[
                    pl.ds(pl.multiple_of(((j - 1) * 2 + c) * SRC_ROWS, SRC_ROWS), SRC_ROWS)
                ],
                me_send,
                me_recv,
                dom,
                h,
            ).start()
        return 0

    lax.fori_loop(1, PLANE, send_meta, 0)
    got_meta[pl.ds(31 * SRC_ROWS, SRC_ROWS), :] = sent_meta[pl.ds(15 * SRC_ROWS, SRC_ROWS), :]

    for copy in ocean_copies:
        copy.wait()
    wide[...] = jnp.zeros_like(wide)
    for e in range(EXT):
        wide[e, 0:HALF, :] = raw[0, :, e * BLK : (e + 1) * BLK]
        wide[e, 16 : 16 + HALF, :] = raw[1, :, e * BLK : (e + 1) * BLK]
    gw_in.wait()

    first_block = d * NB - NH

    def gradient(i, _):
        b = c * (NB // 2) + i
        picked = jnp.concatenate(
            [wide[jnp.maximum(nb_ref[b, k] - first_block, 0)] for k in range(4)], axis=1
        )
        grads[b] = jnp.dot(picked, gw[i], preferred_element_type=jnp.float32).astype(
            jnp.bfloat16
        )
        return 0

    lax.fori_loop(0, NB // 2, gradient, 0, unroll=4)
    mine = pl.ds(c * (NB // 2), NB // 2)
    grad_copy = remote(grads.at[mine], grads.at[mine], gr_send, gr_recv, d, other)
    grad_copy.start()

    all_but_own = pl.ds(0, 31 * SRC_ROWS)
    pltpu.make_async_copy(got_meta.at[all_but_own], got_meta.at[all_but_own], me_recv).wait()
    rows_all = 32 * SRC_ROWS
    lane = lax.broadcasted_iota(jnp.int32, (rows_all, NZ * SLOTS), 1)
    row = lax.broadcasted_iota(jnp.int32, (rows_all, NZ * SLOTS), 0)
    wanted = (lax.rem(lane, SLOTS) + 1).astype(jnp.float32)
    same_z = lax.div(lax.rem(row, SRC_ROWS), 2) == lax.div(lane, SLOTS)
    chosen = jnp.where(
        same_z & (got_meta[...].astype(jnp.float32) == wanted), 1.0, 0.0
    )
    select[...] = chosen.T.astype(jnp.bfloat16)

    rw_in.wait()
    grad_copy.wait()

    own_block = d * NB

    def remap(t, _):
        s = jnp.maximum(src_ref[0, t] - own_block, 0)
        source = jnp.concatenate([wide[s + NH], grads[s]], axis=1)
        cont[pl.ds(pl.multiple_of(t * PITCH, 8), 32), :] = jnp.dot(
            source, rw[t], preferred_element_type=jnp.float32
        )
        return 0

    lax.fori_loop(0, TILES, remap, 0, unroll=8)

    def turn(g, _):
        for h in range(2):
            fields[h * HALF + g] = cont[pl.ds(h * 16 + g, TILES, stride=PITCH), :].astype(
                jnp.bfloat16
            )
        return 0

    own_rows = pl.ds(15 * SRC_ROWS, SRC_ROWS)
    for k in range(CHUNKS):
        lax.fori_loop(k * FCH, (k + 1) * FCH, turn, 0, unroll=True)
        for h in range(2):
            for g in range(k * FCH, (k + 1) * FCH):
                f = h * HALF + g
                sent[f] = jnp.dot(
                    pack[...], fields[f], preferred_element_type=jnp.float32
                ).astype(jnp.bfloat16)
        chunk = pl.ds(k * FCH, FCH)

        remote(
            sent.at[pl.ds(other * HALF + k * FCH, FCH), own_rows],
            got.at[chunk, pl.ds(30 * SRC_ROWS, SRC_ROWS)],
            pl_send.at[k],
            pl_recv.at[k],
            d,
            other,
        ).start()

        def send(j, _, k=k, chunk=chunk):
            dom = plane_chip(j)
            for h in range(2):
                remote(
                    sent.at[
                        pl.ds(h * HALF + k * FCH, FCH),
                        pl.ds(pl.multiple_of((j - 1) * SRC_ROWS, SRC_ROWS), SRC_ROWS),
                    ],
                    got.at[
                        chunk,
                        pl.ds(pl.multiple_of(((j - 1) * 2 + c) * SRC_ROWS, SRC_ROWS), SRC_ROWS),
                    ],
                    pl_send.at[k],
                    pl_recv.at[k],
                    dom,
                    h,
                ).start()
            return 0

        lax.fori_loop(1, PLANE, send, 0)
        got[chunk, pl.ds(31 * SRC_ROWS, SRC_ROWS), :] = sent[
            pl.ds(c * HALF + k * FCH, FCH), own_rows, :
        ]

    for k in range(CHUNKS):
        chunk = pl.ds(k * FCH, FCH)
        arrived = got.at[chunk, all_but_own]
        pltpu.make_async_copy(arrived, arrived, pl_recv.at[k]).wait()
        for g in range(k * FCH, (k + 1) * FCH):
            total = jnp.dot(select[...], got[g], preferred_element_type=jnp.float32)
            own[g] = total[0:SLOTS]
            part[g] = total.astype(jnp.bfloat16)

        def send_z(dz, _, k=k, chunk=chunk):
            remote(
                part.at[chunk, pl.ds(pl.multiple_of(dz * SLOTS, SLOTS), SLOTS)],
                zgot.at[chunk, pl.ds(pl.multiple_of((dz - 1) * SLOTS, SLOTS), SLOTS)],
                z_send.at[k],
                z_recv.at[k],
                line_chip(dz),
                c,
            ).start()
            return 0

        lax.fori_loop(1, NZ, send_z, 0)

    for k in range(CHUNKS):
        chunk = pl.ds(k * FCH, FCH)
        pltpu.make_async_copy(zgot.at[chunk], zgot.at[chunk], z_recv.at[k]).wait()
        for g in range(k * FCH, (k + 1) * FCH):
            total = own[g]
            for s in range(NZ - 1):
                total = total + zgot[g, s * SLOTS : (s + 1) * SLOTS, :].astype(jnp.float32)
            last[g * OPITCH : g * OPITCH + SLOTS, :] = total
    last[HALF * OPITCH :, :] = jnp.zeros((OPITCH, BLK), jnp.float32)
    for s in range(SLOTS):
        line = last[pl.ds(s, 16, stride=OPITCH), :]
        out_ref[:, s * BLK : (s + 1) * BLK] = line[0:HALF]

    pltpu.make_async_copy(got_meta.at[all_but_own], got_meta.at[all_but_own], me_send).wait()
    for k in range(CHUNKS):
        chunk = pl.ds(k * FCH, FCH)
        arrived = got.at[chunk, all_but_own]
        pltpu.make_async_copy(arrived, arrived, pl_send.at[k]).wait()
        pltpu.make_async_copy(zgot.at[chunk], zgot.at[chunk], z_send.at[k]).wait()


def local(ocean, grad_weight, neighbours, remap_weight, tile_src, tile_atm, atm_owner):
    x, z, y = coords()
    slot = jnp.sum(
        jnp.where(
            tile_atm[:, None] == jnp.arange(atm_owner.shape[0], dtype=jnp.int32)[None, :],
            atm_owner[None, :],
            0,
        ),
        axis=1,
    )
    owner, local_slot = slot // SLOTS, slot % SLOTS
    order = jnp.arange(TILES, dtype=jnp.int32)
    rank = jnp.sum(
        ((owner[:, None] == owner[None, :]) & (order[:, None] < order[None, :])).astype(jnp.int32),
        axis=0,
    )
    ox, oz, oy = owner // (NZ * NY), (owner // NY) % NZ, owner % NY
    j = ((ox - x) % NX) * NY + (oy - y) % NY
    rows = ((j + 15) % 16) * SRC_ROWS + ((oz - z) % NZ) * 2 + rank
    meta = jnp.broadcast_to((local_slot + 1).astype(jnp.bfloat16)[:, None], (TILES, BLK))
    bf16, f32 = jnp.bfloat16, jnp.float32
    vmem, smem, hbm = (
        pl.BlockSpec(memory_space=pltpu.VMEM),
        pl.BlockSpec(memory_space=pltpu.SMEM),
        pl.BlockSpec(memory_space=pl.ANY),
    )
    dma = pltpu.SemaphoreType.DMA
    return pl.pallas_call(
        kernel,
        out_shape=jax.ShapeDtypeStruct((HALF, NB * BLK), f32),
        in_specs=[hbm, hbm, smem, hbm, smem, vmem, vmem],
        out_specs=vmem,
        scratch_shapes=[
            pltpu.VMEM((2, HALF, EXT * BLK), bf16),
            pltpu.VMEM((EXT, 32, BLK), bf16),
            pltpu.VMEM((NB // 2, 4 * BLK, 2 * BLK), bf16),
            pltpu.VMEM((TILES, 3 * BLK, BLK), bf16),
            pltpu.VMEM((NB, 32, 2 * BLK), bf16),
            pltpu.VMEM((TILES * PITCH, BLK), f32),
            pltpu.VMEM((2 * HALF, TILES, BLK), bf16),
            pltpu.VMEM((PLANE * SRC_ROWS, TILES), bf16),
            pltpu.VMEM((2 * HALF, PLANE * SRC_ROWS, BLK), bf16),
            pltpu.VMEM((PLANE * SRC_ROWS, BLK), bf16),
            pltpu.VMEM((HALF, 32 * SRC_ROWS, BLK), bf16),
            pltpu.VMEM((32 * SRC_ROWS, BLK), bf16),
            pltpu.VMEM((NZ * SLOTS, 32 * SRC_ROWS), bf16),
            pltpu.VMEM((HALF, NZ * SLOTS, BLK), bf16),
            pltpu.VMEM((HALF, SLOTS, BLK), f32),
            pltpu.VMEM((HALF, (NZ - 1) * SLOTS, BLK), bf16),
            pltpu.VMEM((16 * OPITCH, BLK), f32),
            dma((2,)),
            dma,
            dma((5,)),
            dma((5,)),
            dma,
            dma,
            dma,
            dma,
            dma((CHUNKS,)),
            dma((CHUNKS,)),
            dma((CHUNKS,)),
            dma((CHUNKS,)),
        ],
        compiler_params=pltpu.CompilerParams(
            collective_id=0, has_side_effects=True, vmem_limit_bytes=40 * 1024 * 1024
        ),
    )(
        ocean,
        grad_weight.reshape(NB, 4 * BLK, 2 * BLK),
        neighbours,
        remap_weight,
        tile_src[None, :],
        rows[None, :],
        meta,
    )


def solution(mesh):
    in_specs = (
        P("field", "dom"),
        P("dom", None, None, None),
        P("dom", None),
        P(("dom", "field"), None, None),
        P(("dom", "field")),
        P(("dom", "field")),
        P(),
    )
    out_specs = P("field", "dom")
    return jax.shard_map(local, mesh=mesh, in_specs=in_specs, out_specs=out_specs, check_vma=False)
```

time: 119 us -> 59.3 us (0.50)
  waiting for transfers between devices: 50.2 us -> 0 us
  Pallas kernels: 0 us -> 49.8 us
  starting transfers between devices: 33.3 us -> 0 us
  blocking collectives: 12.3 us -> 0 us
  matrix products: 7.59 us -> 0 us
  other arithmetic: 7.06 us -> 1.07 us
    all_to_all x2 -> x0, waiting for transfers between devices: 50.2 us -> none  [the longest x1 47.7 us: deliver(): lax.all_to_all(outgoing.astype(jnp.bfloat16), 'dom', split_axis=0, concat...]
    pallas_call x0 -> x1, Pallas kernels: none -> 49.8 us  [local(): pl.pallas_call(kernel, out_shape=jax.ShapeDtypeStruct((HALF, NB * BLK), f...]
    all_to_all x2 -> x0, starting transfers between devices: 28 us -> none  [the longest x1 17.3 us: deliver(): lax.all_to_all(targets, 'dom', split_axis=0, concat_axis=0, tiled=True)]
    all_to_all x2 -> x0, blocking collectives: 12.3 us -> none  [the longest x1 7.74 us: summed_on_arrival(): lax.all_to_all(parts, axis, split_axis=0, concat_axis=0, tiled=True)]
    dot_general x3 -> x0, matrix products: 7.59 us -> none  [the longest x1 4.05 us: local(): jnp.einsum('ftj,tjc->tfc', source_rows, remap_weight, preferred_element_t...]
    unnamed x2 -> x10, local copies, waits for them, and re-layouts: 0.88 us -> 7.89 us
    ppermute x2 -> x0, starting transfers between devices: 5.3 us -> none  [the longest x1 4.01 us: padded_2(): before = lax.ppermute(last, axis, up)]
    gather x4 -> x0, local copies, waits for them, and re-layouts: 4.39 us -> none  [the longest x1 1.87 us: deliver(): targets = jnp.where(filled, local_slot[chosen], -1)]
  transfers between devices with their start and end apart: 4 -> 0, of which waited for: 2 -> 0; matrix products, arithmetic and copies ran while one was open for 14% -> 0% of each run, Pallas kernels for 0% -> 0%
where the time goes in v1:
time: 59.3 us; the launch traced here: 58.9 us
  Pallas kernels  49.8 us (84%)
  local copies, waits for them, and re-layouts  7.96 us (13%)
  other arithmetic  1.07 us (2%)
    pallas_call x1, Pallas kernels, local(): pl.pallas_call(kernel, out_shape=jax.ShapeDtypeStruct((HALF, NB * BLK), f...  49.8 us
    unnamed x10, local copies, waits for them, and re-layouts  7.89 us

profile of v1, /device:TPU:1, one launch (start us, length us, event | category | flops | bytes accessed | tf_op | source)
XLA Modules:
  0.0 58.9 jit_solution(15151638109496005865)
XLA Ops:
  0.0 0.9 %select_reduce_fusion = s32[64]{0:T(128)S(1)} fusion(s32[2048]{0:T(1024)} %param.13, s32[64]{0:T(128)} %param.12), kind=kLoop, calls=%fused_computation | loop fusion | flops 393152 | bytes 8704 | tf_op jit(solution)/shard_map/reduce_sum | solution.py:334
  0.9 0.1 convert_reduce_fusion
  1.1 0.8 %copy.9.nb_ref = s32[16,4]{1,0:T(8,128)S(1)} copy(s32[16,4]{0,1:T(4,128)} %param.9) | data formatting | bytes 512 | tf_op args[2]
  1.8 0.1 broadcast_in_dim.19.meta_ref
  1.9 0.0 copy-start
  1.9 2.8 %copy-done = bf16[64,384,128]{2,1,0:T(8,128)(2,1)S(1)} copy-done((bf16[64,384,128]{2,1,0:T(8,128)(2,1)S(1)}, bf16[64,384,128]{2,1,0:T(8,128)(2,1)}, u32[]{:S(2)}) %copy-start) | copy-done | bytes 6291480
  4.7 0.0 copy-start.1
  4.7 2.2 %copy-done.1 = bf16[16,4,128,256]{3,2,1,0:T(8,128)(2,1)S(1)} copy-done((bf16[16,4,128,256]{3,2,1,0:T(8,128)(2,1)S(1)}, bf16[16,4,128,256]{3,2,1,0:T(8,128)(2,1)}, u32[]{:S(2)}) %copy-start.1) | copy-done | bytes 4194328
  6.9 0.0 copy-start.2
  6.9 0.8 %copy-done.2 = bf16[15,2048]{1,0:T(8,128)(2,1)S(1)} copy-done((bf16[15,2048]{1,0:T(8,128)(2,1)S(1)}, bf16[15,2048]{1,0:T(8,128)(2,1)}, u32[]{:S(2)}) %copy-start.2) | copy-done | bytes 61464
  7.7 0.0 copy-start.3
  7.7 0.7 %copy-done.3 = s32[64]{0:T(128)S(1)} copy-done((s32[64]{0:T(128)S(1)}, s32[64]{0:T(128)}, u32[]{:S(2)}) %copy-start.3) | copy-done | bytes 280
  8.4 49.8 %shard_map.73 = f32[15,2048]{1,0:T(8,128)S(1)} custom-call(bf16[15,2048]{1,0:T(8,128)(2,1)S(1)} %copy-done.2, bf16[16,512,256]{2,1,0:T(8,128)(2,1)S(1)} %bitcast.14, s32[16,4]{1,0:T(8,128)S(1)} %copy.9.nb_ref, bf16[64,384,128]{2,1,0:T(8,128)(2,1)S(1)} %copy-done, s32[1,64]{1,0:T(1,128)S(1)} %bitcast.15, s32[1,64]{1,0:T(1,128)S(1)} %fusion.6.rows_ref, ...), custom_call_target="tpu_custom_call" | custom-call | tf_op jit(solution)/shard_map/pallas_call | solution.py:359
  58.2 0.7 %copy.11 = f32[15,2048]{1,0:T(8,128)} copy(f32[15,2048]{1,0:T(8,128)S(1)} %shard_map.73) | data formatting | bytes 245760
  (2 shorter events, 0.1 us)
Async XLA Ops:
  1.9 2.8 %copy-start = (bf16[64,384,128]{2,1,0:T(8,128)(2,1)S(1)}, bf16[64,384,128]{2,1,0:T(8,128)(2,1)}, u32[]{:S(2)}) copy-start(bf16[64,384,128]{2,1,0:T(8,128)(2,1)} %rw_hbm.1) | copy-start | bytes 18874372
  4.7 2.2 %copy-start.1 = (bf16[16,4,128,256]{3,2,1,0:T(8,128)(2,1)S(1)}, bf16[16,4,128,256]{3,2,1,0:T(8,128)(2,1)}, u32[]{:S(2)}) copy-start(bf16[16,4,128,256]{3,2,1,0:T(8,128)(2,1)} %param.8) | copy-start | bytes 12582916
  6.9 0.8 %copy-start.2 = (bf16[15,2048]{1,0:T(8,128)(2,1)S(1)}, bf16[15,2048]{1,0:T(8,128)(2,1)}, u32[]{:S(2)}) copy-start(bf16[15,2048]{1,0:T(8,128)(2,1)} %ocean_hbm.1) | copy-start | bytes 184324
  7.7 0.7 %copy-start.3 = (s32[64]{0:T(128)S(1)}, s32[64]{0:T(128)}, u32[]{:S(2)}) copy-start(s32[64]{0:T(128)} %param.11) | copy-start | bytes 772

commit v2 on v1

--- a/solution.py
+++ b/solution.py
@@ -36,12 +36,16 @@
 def kernel(
     ocean_hbm,
     gw_hbm,
+    nb_hbm,
+    rw_hbm,
+    src_hbm,
+    atm_hbm,
+    owner_hbm,
+    out_ref,
     nb_ref,
-    rw_hbm,
     src_ref,
-    rows_ref,
-    meta_ref,
-    out_ref,
+    atm,
+    owners,
     raw,
     wide,
     gw,
@@ -63,8 +67,7 @@
     w_sem,
     oc_send,
     oc_recv,
-    gr_send,
-    gr_recv,
+    near_sem,
     me_send,
     me_recv,
     pl_send,
@@ -89,46 +92,75 @@
         ocean_hbm, raw.at[c, :, pl.ds(NH * BLK, NB * BLK)], load_sem.at[0]
     )
     ocean_in.start()
-    gw_in = pltpu.make_async_copy(
-        gw_hbm.at[pl.ds(c * (NB // 2), NB // 2)], gw, load_sem.at[1]
-    )
+    small = [
+        pltpu.make_async_copy(src, dst, load_sem.at[n])
+        for n, (src, dst) in enumerate(
+            ((atm_hbm, atm), (owner_hbm, owners), (nb_hbm, nb_ref), (src_hbm, src_ref)), 1
+        )
+    ]
+    for copy in small:
+        copy.start()
+    gw_in = pltpu.make_async_copy(gw_hbm, gw, load_sem.at[5])
     gw_in.start()
     rw_in = pltpu.make_async_copy(rw_hbm, rw, w_sem)
     rw_in.start()
 
     barrier = pltpu.get_barrier_semaphore()
 
-    def greet(dom, core):
+    def greet(dom, core, sem=barrier):
         pl.semaphore_signal(
-            barrier, inc=1, device_id={"dom": dom, "field": core}, device_id_type=MESH
-        )
-
-    greet(d, other)
+            sem, inc=1, device_id={"dom": dom, "field": core}, device_id_type=MESH
+        )
+
+    y_ring = [chip(x, z, lax.rem(y + n, NY)) for n in range(1, NY)]
+    z_near = [chip(x, lax.rem(z + n, NZ), y) for n in (1, NZ - 1, 2, NZ - 2)]
     for h in range(2):
         greet(up, h)
         greet(down, h)
-
-    def greet_plane(j, _):
-        greet(plane_chip(j), 0)
-        greet(plane_chip(j), 1)
-        return 0
-
-    lax.fori_loop(1, PLANE, greet_plane, 0)
-
-    def greet_line(dz, _):
-        greet(line_chip(dz), c)
-        return 0
-
-    lax.fori_loop(1, NZ, greet_line, 0)
-
-    target = rows_ref[...]
-    row_of = lax.broadcasted_iota(jnp.int32, (PLANE * SRC_ROWS, TILES), 0)
-    pack[...] = jnp.where(row_of == target, 1.0, 0.0).astype(jnp.bfloat16)
-    packed_meta = jnp.dot(pack[...], meta_ref[...], preferred_element_type=jnp.float32)
-    sent_meta[...] = packed_meta.astype(jnp.bfloat16)
+    for dom in z_near + y_ring:
+        greet(dom, c)
+    for n in range(1, NX):
+        for h in range(2):
+            greet(chip(lax.rem(x + n, NX), z, y), h)
+    greet(d, other)
+
+    small[0].wait()
+    small[1].wait()
+    bf16, f32 = jnp.bfloat16, jnp.float32
+
+    def dot(a, b):
+        return jnp.dot(a, b, preferred_element_type=f32)
+
+    def iota(shape, dim):
+        return lax.broadcasted_iota(jnp.int32, shape, dim)
+
+    def one_hot(mask):
+        return jnp.where(mask, 1.0, 0.0).astype(bf16)
+
+    ids = atm[...]
+    table = owners[...]
+    halves = jnp.concatenate([table >> 4, table & 15], axis=0).astype(f32).astype(bf16)
+    found = dot(halves, one_hot(iota((BLK, TILES), 0) == (ids & (BLK - 1))))
+    here = iota((16, TILES), 0) == (ids >> 7)
+    owner_row = jnp.sum(jnp.where(here, found[0:16], 0.0), axis=0, keepdims=True)
+    slot_row = jnp.sum(jnp.where(here, found[16:32], 0.0), axis=0, keepdims=True)
+    square = (TILES, TILES)
+    diagonal = jnp.where(iota(square, 0) == iota(square, 1), owner_row, 0.0).astype(bf16)
+    owner_col = dot(diagonal, jnp.ones(square, bf16))
+    earlier = (owner_col == owner_row) & (iota(square, 0) < iota(square, 1))
+    rank = jnp.sum(jnp.where(earlier, 1, 0), axis=0, keepdims=True)
+    owner = owner_row.astype(jnp.int32)
+    dx = ((owner >> 5) - x) & (NX - 1)
+    dz = ((owner >> 2) - z) & (NZ - 1)
+    dy = (owner - y) & (NY - 1)
+    target = ((dx * NY + dy + PLANE - 1) & (PLANE - 1)) * SRC_ROWS + dz * 2 + rank
+    chosen = iota((PLANE * SRC_ROWS, TILES), 0) == target
+    pack[...] = one_hot(chosen)
+    slots_at = jnp.where(chosen, slot_row + 1.0, 0.0).astype(bf16)
+    sent_meta[...] = dot(slots_at, jnp.ones((TILES, BLK), bf16)).astype(bf16)
     ocean_in.wait()
 
-    pl.semaphore_wait(barrier, 1 + 4 + 2 * (PLANE - 1) + (NZ - 1))
+    pl.semaphore_wait(barrier, 4 + 4 + 3 + 6 + 1)
 
     def remote(src, dst, send, recv, dom, core):
         return pltpu.make_async_remote_copy(
@@ -155,6 +187,10 @@
     for copy in ocean_copies:
         copy.start()
 
+    for dom in y_ring + z_near[2:]:
+        greet(dom, c, near_sem)
+    pl.semaphore_wait(near_sem, 5)
+
     meta_partner = remote(
         sent_meta.at[pl.ds(15 * SRC_ROWS, SRC_ROWS)],
         got_meta.at[pl.ds(30 * SRC_ROWS, SRC_ROWS)],
@@ -193,35 +229,29 @@
 
     first_block = d * NB - NH
 
-    def gradient(i, _):
-        b = c * (NB // 2) + i
+    small[2].wait()
+    small[3].wait()
+
+    def gradient(b, _):
         picked = jnp.concatenate(
-            [wide[jnp.maximum(nb_ref[b, k] - first_block, 0)] for k in range(4)], axis=1
-        )
-        grads[b] = jnp.dot(picked, gw[i], preferred_element_type=jnp.float32).astype(
+            [wide[jnp.maximum(nb_ref[k, b] - first_block, 0)] for k in range(4)], axis=1
+        )
+        grads[b] = jnp.dot(picked, gw[b], preferred_element_type=jnp.float32).astype(
             jnp.bfloat16
         )
         return 0
 
-    lax.fori_loop(0, NB // 2, gradient, 0, unroll=4)
-    mine = pl.ds(c * (NB // 2), NB // 2)
-    grad_copy = remote(grads.at[mine], grads.at[mine], gr_send, gr_recv, d, other)
-    grad_copy.start()
-
+    lax.fori_loop(0, NB, gradient, 0, unroll=4)
     all_but_own = pl.ds(0, 31 * SRC_ROWS)
     pltpu.make_async_copy(got_meta.at[all_but_own], got_meta.at[all_but_own], me_recv).wait()
     rows_all = 32 * SRC_ROWS
-    lane = lax.broadcasted_iota(jnp.int32, (rows_all, NZ * SLOTS), 1)
-    row = lax.broadcasted_iota(jnp.int32, (rows_all, NZ * SLOTS), 0)
-    wanted = (lax.rem(lane, SLOTS) + 1).astype(jnp.float32)
-    same_z = lax.div(lax.rem(row, SRC_ROWS), 2) == lax.div(lane, SLOTS)
-    chosen = jnp.where(
-        same_z & (got_meta[...].astype(jnp.float32) == wanted), 1.0, 0.0
-    )
-    select[...] = chosen.T.astype(jnp.bfloat16)
+    lane, row = iota((rows_all, NZ * SLOTS), 1), iota((rows_all, NZ * SLOTS), 0)
+    wanted = ((lane & (SLOTS - 1)) + 1).astype(f32)
+    same_z = ((row & (SRC_ROWS - 1)) >> 1) == (lane >> 4)
+    chosen = jnp.where(same_z & (got_meta[...].astype(f32) == wanted), 1.0, 0.0)
+    select[...] = chosen.T.astype(bf16)
 
     rw_in.wait()
-    grad_copy.wait()
 
     own_block = d * NB
 
@@ -330,41 +360,23 @@
 
 
 def local(ocean, grad_weight, neighbours, remap_weight, tile_src, tile_atm, atm_owner):
-    x, z, y = coords()
-    slot = jnp.sum(
-        jnp.where(
-            tile_atm[:, None] == jnp.arange(atm_owner.shape[0], dtype=jnp.int32)[None, :],
-            atm_owner[None, :],
-            0,
-        ),
-        axis=1,
-    )
-    owner, local_slot = slot // SLOTS, slot % SLOTS
-    order = jnp.arange(TILES, dtype=jnp.int32)
-    rank = jnp.sum(
-        ((owner[:, None] == owner[None, :]) & (order[:, None] < order[None, :])).astype(jnp.int32),
-        axis=0,
-    )
-    ox, oz, oy = owner // (NZ * NY), (owner // NY) % NZ, owner % NY
-    j = ((ox - x) % NX) * NY + (oy - y) % NY
-    rows = ((j + 15) % 16) * SRC_ROWS + ((oz - z) % NZ) * 2 + rank
-    meta = jnp.broadcast_to((local_slot + 1).astype(jnp.bfloat16)[:, None], (TILES, BLK))
-    bf16, f32 = jnp.bfloat16, jnp.float32
-    vmem, smem, hbm = (
-        pl.BlockSpec(memory_space=pltpu.VMEM),
-        pl.BlockSpec(memory_space=pltpu.SMEM),
-        pl.BlockSpec(memory_space=pl.ANY),
-    )
+    bf16, f32, i32 = jnp.bfloat16, jnp.float32, jnp.int32
+    vmem = pl.BlockSpec(memory_space=pltpu.VMEM)
+    hbm = pl.BlockSpec(memory_space=pltpu.HBM)
     dma = pltpu.SemaphoreType.DMA
     return pl.pallas_call(
         kernel,
         out_shape=jax.ShapeDtypeStruct((HALF, NB * BLK), f32),
-        in_specs=[hbm, hbm, smem, hbm, smem, vmem, vmem],
+        in_specs=[hbm] * 7,
         out_specs=vmem,
         scratch_shapes=[
+            pltpu.SMEM((4, NB), i32),
+            pltpu.SMEM((1, TILES), i32),
+            pltpu.VMEM((1, TILES), i32),
+            pltpu.VMEM((NB, BLK), i32),
             pltpu.VMEM((2, HALF, EXT * BLK), bf16),
             pltpu.VMEM((EXT, 32, BLK), bf16),
-            pltpu.VMEM((NB // 2, 4 * BLK, 2 * BLK), bf16),
+            pltpu.VMEM((NB, 4 * BLK, 2 * BLK), bf16),
             pltpu.VMEM((TILES, 3 * BLK, BLK), bf16),
             pltpu.VMEM((NB, 32, 2 * BLK), bf16),
             pltpu.VMEM((TILES * PITCH, BLK), f32),
@@ -379,12 +391,11 @@
             pltpu.VMEM((HALF, SLOTS, BLK), f32),
             pltpu.VMEM((HALF, (NZ - 1) * SLOTS, BLK), bf16),
             pltpu.VMEM((16 * OPITCH, BLK), f32),
-            dma((2,)),
+            dma((6,)),
             dma,
             dma((5,)),
             dma((5,)),
-            dma,
-            dma,
+            pltpu.SemaphoreType.REGULAR,
             dma,
             dma,
             dma((CHUNKS,)),
@@ -393,16 +404,16 @@
             dma((CHUNKS,)),
         ],
         compiler_params=pltpu.CompilerParams(
-            collective_id=0, has_side_effects=True, vmem_limit_bytes=40 * 1024 * 1024
+            collective_id=0, has_side_effects=True, vmem_limit_bytes=67_043_328
         ),
     )(
         ocean,
         grad_weight.reshape(NB, 4 * BLK, 2 * BLK),
-        neighbours,
+        neighbours.T,
         remap_weight,
         tile_src[None, :],
-        rows[None, :],
-        meta,
+        tile_atm[None, :],
+        atm_owner.reshape(NB, BLK),
     )
 
 

time: 59.3 us -> 52.2 us (0.88)
  local copies, waits for them, and re-layouts: 7.96 us -> 1.57 us
  other arithmetic: 1.07 us -> 0 us
  Pallas kernels: 49.8 us -> 50.5 us
    unnamed x10 -> x1, local copies, waits for them, and re-layouts: 7.89 us -> 1.57 us
    reduce_sum x2 -> x0, other arithmetic: 1.02 us -> none  [the longest x1 0.92 us: local(): jnp.sum(jnp.where(tile_atm[:, None] == jnp.arange(atm_owner.shape[0], dty...]
    pallas_call x1, Pallas kernels: 49.8 us -> 50.5 us  [local(): pl.pallas_call(kernel, out_shape=jax.ShapeDtypeStruct((HALF, NB * BLK), f...]
where the time goes in v2:
time: 52.2 us; the launch traced here: 52.1 us
  Pallas kernels  50.5 us (97%)
  local copies, waits for them, and re-layouts  1.57 us (3%)
    pallas_call x1, Pallas kernels, local(): pl.pallas_call(kernel, out_shape=jax.ShapeDtypeStruct((HALF, NB * BLK), f...  50.5 us
    unnamed x1, local copies, waits for them, and re-layouts  1.57 us

profile of v2, /device:TPU:1, one launch (start us, length us, event | category | flops | bytes accessed | tf_op | source)
XLA Modules:
  0.0 52.1 jit_solution(1928595765211416842)
XLA Ops:
  0.0 50.5 %shard_map.73 = f32[15,2048]{1,0:T(8,128)} custom-call(bf16[15,2048]{1,0:T(8,128)(2,1)} %ocean_hbm.1, bf16[16,512,256]{2,1,0:T(8,128)(2,1)} %bitcast.5, s32[4,16]{1,0:T(4,128)} %bitcast.7, bf16[64,384,128]{2,1,0:T(8,128)(2,1)} %rw_hbm.1, s32[1,64]{1,0:T(1,128)} %bitcast.8, s32[1,64]{1,0:T(1,128)} %bitcast.9, s32[16,128]{1,0:T(8,128)} %bitcast.6), custom_call_target="tpu_custom_call" | custom-call | tf_op jit(solution)/shard_map/pallas_call | solution.py:367
  50.5 1.6 %copy.9 = f32[15,2048]{1,0:T(8,128)} copy(f32[15,2048]{1,0:T(8,128)} %shard_map.73) | data formatting | bytes 245760

commit v3 on v2

--- a/solution.py
+++ b/solution.py
@@ -18,8 +18,9 @@
 TILES = 64
 SLOTS = 16
 SRC_ROWS = 16
-FCH = 3
-CHUNKS = HALF // FCH
+SPLIT = ((0, 3), (3, 3), (6, 3), (9, 2), (11, 1))
+CHUNKS = len(SPLIT)
+ZF, ZN = 12, 3
 PITCH = 40
 OPITCH = 24
 
@@ -63,6 +64,15 @@
     own,
     zgot,
     last,
+    zpack,
+    zsent,
+    zsent_meta,
+    zraw,
+    zraw_meta,
+    zselect,
+    zpart,
+    zown,
+    zlast,
     load_sem,
     w_sem,
     oc_send,
@@ -74,6 +84,12 @@
     pl_recv,
     z_send,
     z_recv,
+    zm_send,
+    zm_recv,
+    zr_send,
+    zr_recv,
+    zp_send,
+    zp_recv,
 ):
     c = lax.axis_index("field")
     d = lax.axis_index("dom")
@@ -117,7 +133,10 @@
     for h in range(2):
         greet(up, h)
         greet(down, h)
-    for dom in z_near + y_ring:
+    for dom in z_near:
+        greet(dom, 0)
+        greet(dom, 1)
+    for dom in y_ring:
         greet(dom, c)
     for n in range(1, NX):
         for h in range(2):
@@ -153,14 +172,25 @@
     dx = ((owner >> 5) - x) & (NX - 1)
     dz = ((owner >> 2) - z) & (NZ - 1)
     dy = (owner - y) & (NY - 1)
-    target = ((dx * NY + dy + PLANE - 1) & (PLANE - 1)) * SRC_ROWS + dz * 2 + rank
-    chosen = iota((PLANE * SRC_ROWS, TILES), 0) == target
-    pack[...] = one_hot(chosen)
-    slots_at = jnp.where(chosen, slot_row + 1.0, 0.0).astype(bf16)
-    sent_meta[...] = dot(slots_at, jnp.ones((TILES, BLK), bf16)).astype(bf16)
+    jj = (dx * NY + dy + PLANE - 1) & (PLANE - 1)
+    z_rel = (dz + NZ - 1) & (NZ - 1)
+    within = (dz * 2 + rank, jj * 2 + rank)
+    plans = (
+        (jj, within[0], SRC_ROWS, pack, sent_meta),
+        (z_rel, within[1], 2 * PLANE, zpack, zsent_meta),
+    )
+    for group, inner, width, matrix, metas in plans:
+        matrix[...] = one_hot(iota((PLANE * SRC_ROWS, TILES), 0) == group * width + inner)
+        marked = jnp.where(iota((PLANE, TILES), 0) == group, slot_row + 1.0, 0.0).astype(bf16)
+        spread = jnp.where(iota(square, 0) == iota(square, 1), inner.astype(f32), 0.0)
+        inner_col = dot(spread.astype(bf16), jnp.ones((TILES, BLK), bf16))
+        lanes = (iota((TILES, BLK), 1) & (width - 1)).astype(f32)
+        table = dot(marked, one_hot(inner_col == lanes))
+        for n in range(metas.shape[0]):
+            metas[n] = table[n : n + 1]
     ocean_in.wait()
 
-    pl.semaphore_wait(barrier, 4 + 4 + 3 + 6 + 1)
+    pl.semaphore_wait(barrier, 4 + 8 + 3 + 6 + 1)
 
     def remote(src, dst, send, recv, dom, core):
         return pltpu.make_async_remote_copy(
@@ -189,36 +219,6 @@
 
     for dom in y_ring + z_near[2:]:
         greet(dom, c, near_sem)
-    pl.semaphore_wait(near_sem, 5)
-
-    meta_partner = remote(
-        sent_meta.at[pl.ds(15 * SRC_ROWS, SRC_ROWS)],
-        got_meta.at[pl.ds(30 * SRC_ROWS, SRC_ROWS)],
-        me_send,
-        me_recv,
-        d,
-        other,
-    )
-    meta_partner.start()
-
-    def send_meta(j, _):
-        dom = plane_chip(j)
-        for h in range(2):
-            remote(
-                sent_meta.at[pl.ds(pl.multiple_of((j - 1) * SRC_ROWS, SRC_ROWS), SRC_ROWS)],
-                got_meta.at[
-                    pl.ds(pl.multiple_of(((j - 1) * 2 + c) * SRC_ROWS, SRC_ROWS), SRC_ROWS)
-                ],
-                me_send,
-                me_recv,
-                dom,
-                h,
-            ).start()
-        return 0
-
-    lax.fori_loop(1, PLANE, send_meta, 0)
-    got_meta[pl.ds(31 * SRC_ROWS, SRC_ROWS), :] = sent_meta[pl.ds(15 * SRC_ROWS, SRC_ROWS), :]
-
     for copy in ocean_copies:
         copy.wait()
     wide[...] = jnp.zeros_like(wide)
@@ -242,15 +242,6 @@
         return 0
 
     lax.fori_loop(0, NB, gradient, 0, unroll=4)
-    all_but_own = pl.ds(0, 31 * SRC_ROWS)
-    pltpu.make_async_copy(got_meta.at[all_but_own], got_meta.at[all_but_own], me_recv).wait()
-    rows_all = 32 * SRC_ROWS
-    lane, row = iota((rows_all, NZ * SLOTS), 1), iota((rows_all, NZ * SLOTS), 0)
-    wanted = ((lane & (SLOTS - 1)) + 1).astype(f32)
-    same_z = ((row & (SRC_ROWS - 1)) >> 1) == (lane >> 4)
-    chosen = jnp.where(same_z & (got_meta[...].astype(f32) == wanted), 1.0, 0.0)
-    select[...] = chosen.T.astype(bf16)
-
     rw_in.wait()
 
     own_block = d * NB
@@ -272,19 +263,59 @@
             )
         return 0
 
+    pl.semaphore_wait(near_sem, 5)
+
+    remote(sent_meta.at[15], got_meta.at[30], me_send, me_recv, d, other).start()
+    remote(zsent_meta.at[7], zraw_meta.at[14], zm_send, zm_recv, d, other).start()
+
+    def send_meta(j, _):
+        for h in range(2):
+            remote(
+                sent_meta.at[j - 1],
+                got_meta.at[(j - 1) * 2 + c],
+                me_send,
+                me_recv,
+                plane_chip(j),
+                h,
+            ).start()
+        return 0
+
+    def send_zmeta(dz, _):
+        for h in range(2):
+            remote(
+                zsent_meta.at[dz - 1],
+                zraw_meta.at[(dz - 1) * 2 + c],
+                zm_send,
+                zm_recv,
+                line_chip(dz),
+                h,
+            ).start()
+        return 0
+
+    lax.fori_loop(1, PLANE, send_meta, 0)
+    lax.fori_loop(1, NZ, send_zmeta, 0)
+    got_meta[31] = sent_meta[15]
+    zraw_meta[15] = zsent_meta[7]
+
+    def z_rows(start):
+        return pl.ds(pl.multiple_of(start * 32, 32), 32)
+
     own_rows = pl.ds(15 * SRC_ROWS, SRC_ROWS)
-    for k in range(CHUNKS):
-        lax.fori_loop(k * FCH, (k + 1) * FCH, turn, 0, unroll=True)
+    all_but_own = pl.ds(0, 31 * SRC_ROWS)
+    z_but_own = pl.ds(0, 15 * 32)
+    zchunk = pl.ds(ZF, ZN)
+
+    def send_plane(k):
+        f0, fn = SPLIT[k]
+        for g in range(f0, f0 + fn):
+            turn(g, 0)
         for h in range(2):
-            for g in range(k * FCH, (k + 1) * FCH):
+            for g in range(f0, f0 + fn):
                 f = h * HALF + g
-                sent[f] = jnp.dot(
-                    pack[...], fields[f], preferred_element_type=jnp.float32
-                ).astype(jnp.bfloat16)
-        chunk = pl.ds(k * FCH, FCH)
-
+                sent[f] = dot(pack[...], fields[f]).astype(bf16)
+        chunk = pl.ds(f0, fn)
         remote(
-            sent.at[pl.ds(other * HALF + k * FCH, FCH), own_rows],
+            sent.at[pl.ds(other * HALF + f0, fn), own_rows],
             got.at[chunk, pl.ds(30 * SRC_ROWS, SRC_ROWS)],
             pl_send.at[k],
             pl_recv.at[k],
@@ -292,12 +323,12 @@
             other,
         ).start()
 
-        def send(j, _, k=k, chunk=chunk):
+        def send(j, _):
             dom = plane_chip(j)
             for h in range(2):
                 remote(
                     sent.at[
-                        pl.ds(h * HALF + k * FCH, FCH),
+                        pl.ds(h * HALF + f0, fn),
                         pl.ds(pl.multiple_of((j - 1) * SRC_ROWS, SRC_ROWS), SRC_ROWS),
                     ],
                     got.at[
@@ -313,19 +344,74 @@
 
         lax.fori_loop(1, PLANE, send, 0)
         got[chunk, pl.ds(31 * SRC_ROWS, SRC_ROWS), :] = sent[
-            pl.ds(c * HALF + k * FCH, FCH), own_rows, :
+            pl.ds(c * HALF + f0, fn), own_rows, :
         ]
 
-    for k in range(CHUNKS):
-        chunk = pl.ds(k * FCH, FCH)
+    send_plane(0)
+    for g in range(ZF, ZF + ZN):
+        turn(g, 0)
+    for h in range(2):
+        for g in range(ZN):
+            zsent[h * ZN + g] = dot(zpack[...], fields[h * HALF + ZF + g]).astype(bf16)
+    remote(
+        zsent.at[pl.ds(other * ZN, ZN), z_rows(7)],
+        zraw.at[:, z_rows(14)],
+        zr_send,
+        zr_recv,
+        d,
+        other,
+    ).start()
+
+    def send_raw(dz, _):
+        for h in range(2):
+            remote(
+                zsent.at[pl.ds(h * ZN, ZN), z_rows(dz - 1)],
+                zraw.at[:, z_rows((dz - 1) * 2 + c)],
+                zr_send,
+                zr_recv,
+                line_chip(dz),
+                h,
+            ).start()
+        return 0
+
+    lax.fori_loop(1, NZ, send_raw, 0)
+    zraw[:, z_rows(15), :] = zsent[pl.ds(c * ZN, ZN), z_rows(7), :]
+    for k in range(1, CHUNKS):
+        send_plane(k)
+
+    most, z_most = got_meta.at[pl.ds(0, 31)], zraw_meta.at[pl.ds(0, 15)]
+    pltpu.make_async_copy(most, most, me_recv).wait()
+    pltpu.make_async_copy(z_most, z_most, zm_recv).wait()
+    lane = iota((1, BLK), 1)
+    uses = (
+        (got_meta, 8, SRC_ROWS, select, (0,)),
+        (zraw_meta, 4, 2 * PLANE, zselect, (0, BLK)),
+    )
+    for metas, per, width, matrix, offsets in uses:
+        for q in range(4):
+            flat = jnp.zeros((1, BLK), f32)
+            for n in range(per):
+                at = (lane >= n * width) & (lane < (n + 1) * width)
+                flat = jnp.where(at, metas[q * per + n], flat)
+            for offset in offsets:
+                row, col = iota((BLK, BLK), 0) + offset, iota((BLK, BLK), 1)
+                fits = (row >> 4) == ((col & (width - 1)) >> 1)
+                slot = ((row & (SLOTS - 1)) + 1).astype(f32)
+                matrix[offset : offset + BLK, q * BLK : (q + 1) * BLK] = one_hot(
+                    fits & (flat == slot)
+                )
+
+    def from_plane(k):
+        f0, fn = SPLIT[k]
+        chunk = pl.ds(f0, fn)
         arrived = got.at[chunk, all_but_own]
         pltpu.make_async_copy(arrived, arrived, pl_recv.at[k]).wait()
-        for g in range(k * FCH, (k + 1) * FCH):
-            total = jnp.dot(select[...], got[g], preferred_element_type=jnp.float32)
+        for g in range(f0, f0 + fn):
+            total = dot(select[...], got[g])
             own[g] = total[0:SLOTS]
-            part[g] = total.astype(jnp.bfloat16)
-
-        def send_z(dz, _, k=k, chunk=chunk):
+            part[g] = total.astype(bf16)
+
+        def send_z(dz, _):
             remote(
                 part.at[chunk, pl.ds(pl.multiple_of(dz * SLOTS, SLOTS), SLOTS)],
                 zgot.at[chunk, pl.ds(pl.multiple_of((dz - 1) * SLOTS, SLOTS), SLOTS)],
@@ -338,22 +424,57 @@
 
         lax.fori_loop(1, NZ, send_z, 0)
 
-    for k in range(CHUNKS):
-        chunk = pl.ds(k * FCH, FCH)
+    for k in range(CHUNKS - 2):
+        from_plane(k)
+
+    pltpu.make_async_copy(zraw.at[:, z_but_own], zraw.at[:, z_but_own], zr_recv).wait()
+    for g in range(ZN):
+        total = dot(zselect[...], zraw[g])
+        zown[g] = total[15 * SLOTS :]
+        zpart[g] = total.astype(bf16)
+
+    def send_sums(j, _):
+        rows = pl.ds(pl.multiple_of((j - 1) * SLOTS, SLOTS), SLOTS)
+        remote(
+            zpart.at[:, rows], zlast.at[:, rows], zp_send, zp_recv, plane_chip(j), c
+        ).start()
+        return 0
+
+    lax.fori_loop(1, PLANE, send_sums, 0)
+
+    for k in range(CHUNKS - 2, CHUNKS):
+        from_plane(k)
+
+    def from_line(k):
+        f0, fn = SPLIT[k]
+        chunk = pl.ds(f0, fn)
         pltpu.make_async_copy(zgot.at[chunk], zgot.at[chunk], z_recv.at[k]).wait()
-        for g in range(k * FCH, (k + 1) * FCH):
+        for g in range(f0, f0 + fn):
             total = own[g]
             for s in range(NZ - 1):
-                total = total + zgot[g, s * SLOTS : (s + 1) * SLOTS, :].astype(jnp.float32)
+                total = total + zgot[g, s * SLOTS : (s + 1) * SLOTS, :].astype(f32)
             last[g * OPITCH : g * OPITCH + SLOTS, :] = total
+
+    for k in range(CHUNKS - 1):
+        from_line(k)
+    pltpu.make_async_copy(zlast, zlast, zp_recv).wait()
+    for g in range(ZN):
+        total = zown[g]
+        for s in range(PLANE - 1):
+            total = total + zlast[g, s * SLOTS : (s + 1) * SLOTS, :].astype(f32)
+        last[(ZF + g) * OPITCH : (ZF + g) * OPITCH + SLOTS, :] = total
+    from_line(CHUNKS - 1)
     last[HALF * OPITCH :, :] = jnp.zeros((OPITCH, BLK), jnp.float32)
     for s in range(SLOTS):
         line = last[pl.ds(s, 16, stride=OPITCH), :]
         out_ref[:, s * BLK : (s + 1) * BLK] = line[0:HALF]
 
-    pltpu.make_async_copy(got_meta.at[all_but_own], got_meta.at[all_but_own], me_send).wait()
+    pltpu.make_async_copy(most, most, me_send).wait()
+    pltpu.make_async_copy(z_most, z_most, zm_send).wait()
+    pltpu.make_async_copy(zraw.at[:, z_but_own], zraw.at[:, z_but_own], zr_send).wait()
+    pltpu.make_async_copy(zlast, zlast, zp_send).wait()
     for k in range(CHUNKS):
-        chunk = pl.ds(k * FCH, FCH)
+        chunk = pl.ds(*SPLIT[k])
         arrived = got.at[chunk, all_but_own]
         pltpu.make_async_copy(arrived, arrived, pl_send.at[k]).wait()
         pltpu.make_async_copy(zgot.at[chunk], zgot.at[chunk], z_send.at[k]).wait()
@@ -383,14 +504,23 @@
             pltpu.VMEM((2 * HALF, TILES, BLK), bf16),
             pltpu.VMEM((PLANE * SRC_ROWS, TILES), bf16),
             pltpu.VMEM((2 * HALF, PLANE * SRC_ROWS, BLK), bf16),
-            pltpu.VMEM((PLANE * SRC_ROWS, BLK), bf16),
+            pltpu.VMEM((PLANE, 1, BLK), f32),
             pltpu.VMEM((HALF, 32 * SRC_ROWS, BLK), bf16),
-            pltpu.VMEM((32 * SRC_ROWS, BLK), bf16),
+            pltpu.VMEM((32, 1, BLK), f32),
             pltpu.VMEM((NZ * SLOTS, 32 * SRC_ROWS), bf16),
             pltpu.VMEM((HALF, NZ * SLOTS, BLK), bf16),
             pltpu.VMEM((HALF, SLOTS, BLK), f32),
             pltpu.VMEM((HALF, (NZ - 1) * SLOTS, BLK), bf16),
             pltpu.VMEM((16 * OPITCH, BLK), f32),
+            pltpu.VMEM((PLANE * SRC_ROWS, TILES), bf16),
+            pltpu.VMEM((2 * ZN, PLANE * SRC_ROWS, BLK), bf16),
+            pltpu.VMEM((NZ, 1, BLK), f32),
+            pltpu.VMEM((ZN, 32 * SRC_ROWS, BLK), bf16),
+            pltpu.VMEM((2 * NZ, 1, BLK), f32),
+            pltpu.VMEM((PLANE * SLOTS, 32 * SRC_ROWS), bf16),
+            pltpu.VMEM((ZN, PLANE * SLOTS, BLK), bf16),
+            pltpu.VMEM((ZN, SLOTS, BLK), f32),
+            pltpu.VMEM((ZN, (PLANE - 1) * SLOTS, BLK), bf16),
             dma((6,)),
             dma,
             dma((5,)),
@@ -402,18 +532,29 @@
             dma((CHUNKS,)),
             dma((CHUNKS,)),
             dma((CHUNKS,)),
+            dma,
+            dma,
+            dma,
+            dma,
+            dma,
+            dma,
         ],
         compiler_params=pltpu.CompilerParams(
-            collective_id=0, has_side_effects=True, vmem_limit_bytes=67_043_328
+            collective_id=0, has_side_effects=True, vmem_limit_bytes=48 * 1024 * 1024
         ),
     )(
-        ocean,
-        grad_weight.reshape(NB, 4 * BLK, 2 * BLK),
-        neighbours.T,
-        remap_weight,
-        tile_src[None, :],
-        tile_atm[None, :],
-        atm_owner.reshape(NB, BLK),
+        *(
+            pltpu.with_memory_space_constraint(a, pltpu.HBM)
+            for a in (
+                ocean,
+                grad_weight.reshape(NB, 4 * BLK, 2 * BLK),
+                neighbours.T,
+                remap_weight,
+                tile_src[None, :],
+                tile_atm[None, :],
+                atm_owner.reshape(NB, BLK),
+            )
+        )
     )
 
 

time: 52.2 us -> 46.4 us (0.89)
  Pallas kernels: 50.5 us -> 45.7 us
  local copies, waits for them, and re-layouts: 1.57 us -> 0.66 us
    pallas_call x1, Pallas kernels: 50.5 us -> 45.7 us  [local(): pl.pallas_call(kernel, out_shape=jax.ShapeDtypeStruct((HALF, NB * BLK), f...]
    unnamed x1, local copies, waits for them, and re-layouts: 1.57 us -> 0.66 us
where the time goes in v3:
time: 46.4 us
  Pallas kernels  45.7 us (98%)
  local copies, waits for them, and re-layouts  0.66 us (1%)
    pallas_call x1, Pallas kernels, local(): pl.pallas_call(kernel, out_shape=jax.ShapeDtypeStruct((HALF, NB * BLK), f...  45.7 us

profile of v3, /device:TPU:1, one launch (start us, length us, event | category | flops | bytes accessed | tf_op | source)
XLA Modules:
  0.0 46.4 jit_solution(10877544266659200425)
XLA Ops:
  0.0 45.7 %shard_map.73 = f32[15,2048]{1,0:T(8,128)S(1)} custom-call(bf16[15,2048]{1,0:T(8,128)(2,1)} %ocean_hbm.1, bf16[16,512,256]{2,1,0:T(8,128)(2,1)} %bitcast.5, s32[4,16]{1,0:T(4,128)} %bitcast.7, bf16[64,384,128]{2,1,0:T(8,128)(2,1)} %rw_hbm.1, s32[1,64]{1,0:T(1,128)} %bitcast.8, s32[1,64]{1,0:T(1,128)} %bitcast.9, s32[16,128]{1,0:T(8,128)} %bitcast.6), custom_call_target="tpu_custom_call" | custom-call | tf_op jit(solution)/shard_map/pallas_call | solution.py:488
  45.7 0.7 %copy.9 = f32[15,2048]{1,0:T(8,128)} copy(f32[15,2048]{1,0:T(8,128)S(1)} %shard_map.73) | data formatting | bytes 245760

commit v4 on v3

--- a/solution.py
+++ b/solution.py
@@ -48,6 +48,7 @@
     atm,
     owners,
     raw,
+    relay,
     wide,
     gw,
     rw,
@@ -129,6 +130,8 @@
         )
 
     y_ring = [chip(x, z, lax.rem(y + n, NY)) for n in range(1, NY)]
+    ahead = chip(lax.rem(x + 1, NX), z, lax.rem(y + 1, NY))
+    behind = chip(lax.rem(x + NX - 1, NX), z, lax.rem(y + NY - 1, NY))
     z_near = [chip(x, lax.rem(z + n, NZ), y) for n in (1, NZ - 1, 2, NZ - 2)]
     for h in range(2):
         greet(up, h)
@@ -141,6 +144,8 @@
     for n in range(1, NX):
         for h in range(2):
             greet(chip(lax.rem(x + n, NX), z, y), h)
+    greet(ahead, c)
+    greet(behind, c)
     greet(d, other)
 
     small[0].wait()
@@ -190,7 +195,7 @@
             metas[n] = table[n : n + 1]
     ocean_in.wait()
 
-    pl.semaphore_wait(barrier, 4 + 8 + 3 + 6 + 1)
+    pl.semaphore_wait(barrier, 4 + 8 + 3 + 6 + 2 + 1)
 
     def remote(src, dst, send, recv, dom, core):
         return pltpu.make_async_remote_copy(
@@ -207,30 +212,74 @@
     left = pl.ds(0, NH * BLK)
     right = pl.ds((NB + NH) * BLK, NH * BLK)
     middle = pl.ds(NH * BLK, NB * BLK)
-    ocean_copies = [
-        remote(raw.at[c, :, final], raw.at[c, :, left], oc_send.at[0], oc_recv.at[0], up, c),
-        remote(raw.at[c, :, final], raw.at[c, :, left], oc_send.at[1], oc_recv.at[1], up, other),
-        remote(raw.at[c, :, first], raw.at[c, :, right], oc_send.at[2], oc_recv.at[2], down, c),
-        remote(raw.at[c, :, first], raw.at[c, :, right], oc_send.at[3], oc_recv.at[3], down, other),
-        remote(raw.at[c, :, middle], raw.at[c, :, middle], oc_send.at[4], oc_recv.at[4], d, other),
+    half = raw.at[c]
+    upward = [
+        remote(half.at[:, final], half.at[:, left], oc_send.at[n], oc_recv.at[n], up, h)
+        for n, h in enumerate((c, other))
     ]
-    for copy in ocean_copies:
+    downward = [
+        remote(half.at[:, first], half.at[:, right], oc_send.at[2 + n], oc_recv.at[2 + n], down, h)
+        for n, h in enumerate((c, other))
+    ]
+    sideways = remote(
+        half.at[:, middle], half.at[:, middle], oc_send.at[4], oc_recv.at[4], d, other
+    )
+    to_relay = remote(half.at[:, first], relay, oc_send.at[5], oc_recv.at[5], behind, c)
+    below = chip(x, NZ - 1, y)
+    relayed = [
+        remote(relay, half.at[:, right], oc_send.at[6 + n], oc_recv.at[2 + n], below, h)
+        for n, h in enumerate((c, other))
+    ]
+    corner = (z == 0) & (y == 0)
+    relaying = (z == 0) & (y == NY - 1)
+    for copy in upward:
         copy.start()
 
+    @pl.when(corner)
+    def _():
+        to_relay.start()
+
+    @pl.when(jnp.logical_not(corner))
+    def _():
+        for copy in downward:
+            copy.start()
+
+    sideways.start()
     for dom in y_ring + z_near[2:]:
         greet(dom, c, near_sem)
-    for copy in ocean_copies:
-        copy.wait()
+    @pl.when(relaying)
+    def _():
+        to_relay.wait_recv()
+        for copy in relayed:
+            copy.start()
+
+    sideways.wait_recv()
     wide[...] = jnp.zeros_like(wide)
-    for e in range(EXT):
-        wide[e, 0:HALF, :] = raw[0, :, e * BLK : (e + 1) * BLK]
-        wide[e, 16 : 16 + HALF, :] = raw[1, :, e * BLK : (e + 1) * BLK]
-    gw_in.wait()
-
-    first_block = d * NB - NH
-
+
+    def spread_blocks(blocks):
+        for e in blocks:
+            wide[e, 0:HALF, :] = raw[0, :, e * BLK : (e + 1) * BLK]
+            wide[e, 16 : 16 + HALF, :] = raw[1, :, e * BLK : (e + 1) * BLK]
+
+    spread_blocks(range(NH, NH + NB))
     small[2].wait()
     small[3].wait()
+    rw_in.wait()
+    own_block = d * NB
+
+    def remap_values(t, _):
+        s = jnp.maximum(src_ref[0, t] - own_block, 0)
+        cont[pl.ds(pl.multiple_of(t * PITCH, 8), 32), :] = dot(wide[s + NH], rw[t, 0:BLK, :])
+        return 0
+
+    lax.fori_loop(0, TILES, remap_values, 0, unroll=8)
+    for copy in upward + downward:
+        copy.wait_recv()
+    spread_blocks((0, 1, NH + NB, NH + NB + 1))
+
+    gw_in.wait()
+
+    first_block = d * NB - NH
 
     def gradient(b, _):
         picked = jnp.concatenate(
@@ -242,16 +291,10 @@
         return 0
 
     lax.fori_loop(0, NB, gradient, 0, unroll=4)
-    rw_in.wait()
-
-    own_block = d * NB
-
     def remap(t, _):
         s = jnp.maximum(src_ref[0, t] - own_block, 0)
-        source = jnp.concatenate([wide[s + NH], grads[s]], axis=1)
-        cont[pl.ds(pl.multiple_of(t * PITCH, 8), 32), :] = jnp.dot(
-            source, rw[t], preferred_element_type=jnp.float32
-        )
+        at = pl.ds(pl.multiple_of(t * PITCH, 8), 32)
+        cont[at, :] = cont[at, :] + dot(grads[s], rw[t, BLK:, :])
         return 0
 
     lax.fori_loop(0, TILES, remap, 0, unroll=8)
@@ -469,6 +512,24 @@
         line = last[pl.ds(s, 16, stride=OPITCH), :]
         out_ref[:, s * BLK : (s + 1) * BLK] = line[0:HALF]
 
+    for copy in upward:
+        copy.wait_send()
+    sideways.wait_send()
+
+    @pl.when(corner)
+    def _():
+        to_relay.wait_send()
+
+    @pl.when(jnp.logical_not(corner))
+    def _():
+        for copy in downward:
+            copy.wait_send()
+
+    @pl.when(relaying)
+    def _():
+        for copy in relayed:
+            copy.wait_send()
+
     pltpu.make_async_copy(most, most, me_send).wait()
     pltpu.make_async_copy(z_most, z_most, zm_send).wait()
     pltpu.make_async_copy(zraw.at[:, z_but_own], zraw.at[:, z_but_own], zr_send).wait()
@@ -496,6 +557,7 @@
             pltpu.VMEM((1, TILES), i32),
             pltpu.VMEM((NB, BLK), i32),
             pltpu.VMEM((2, HALF, EXT * BLK), bf16),
+            pltpu.VMEM((HALF, NH * BLK), bf16),
             pltpu.VMEM((EXT, 32, BLK), bf16),
             pltpu.VMEM((NB, 4 * BLK, 2 * BLK), bf16),
             pltpu.VMEM((TILES, 3 * BLK, BLK), bf16),
@@ -523,8 +585,8 @@
             pltpu.VMEM((ZN, (PLANE - 1) * SLOTS, BLK), bf16),
             dma((6,)),
             dma,
-            dma((5,)),
-            dma((5,)),
+            dma((8,)),
+            dma((6,)),
             pltpu.SemaphoreType.REGULAR,
             dma,
             dma,

time: 46.4 us -> 47.6 us (1.026)
  Pallas kernels: 45.7 us -> 46.9 us
    pallas_call x1, Pallas kernels: 45.7 us -> 46.9 us  [local(): pl.pallas_call(kernel, out_shape=jax.ShapeDtypeStruct((HALF, NB * BLK), f...]
where the time goes in v4:
time: 47.6 us; the launch traced here: 47.5 us
  Pallas kernels  46.9 us (99%)
  local copies, waits for them, and re-layouts  0.66 us (1%)
    pallas_call x1, Pallas kernels, local(): pl.pallas_call(kernel, out_shape=jax.ShapeDtypeStruct((HALF, NB * BLK), f...  46.9 us

profile of v4, /device:TPU:1, one launch (start us, length us, event | category | flops | bytes accessed | tf_op | source)
XLA Modules:
  0.0 47.5 jit_solution(6283714240468010523)
XLA Ops:
  0.0 46.9 %shard_map.73 = f32[15,2048]{1,0:T(8,128)S(1)} custom-call(bf16[15,2048]{1,0:T(8,128)(2,1)} %ocean_hbm.1, bf16[16,512,256]{2,1,0:T(8,128)(2,1)} %bitcast.5, s32[4,16]{1,0:T(4,128)} %bitcast.7, bf16[64,384,128]{2,1,0:T(8,128)(2,1)} %rw_hbm.1, s32[1,64]{1,0:T(1,128)} %bitcast.8, s32[1,64]{1,0:T(1,128)} %bitcast.9, s32[16,128]{1,0:T(8,128)} %bitcast.6), custom_call_target="tpu_custom_call" | custom-call | tf_op jit(solution)/shard_map/pallas_call | solution.py:549
  46.9 0.7 %copy.9 = f32[15,2048]{1,0:T(8,128)} copy(f32[15,2048]{1,0:T(8,128)S(1)} %shard_map.73) | data formatting | bytes 245760

commit v5 on v4

--- a/solution.py
+++ b/solution.py
@@ -18,9 +18,9 @@
 TILES = 64
 SLOTS = 16
 SRC_ROWS = 16
-SPLIT = ((0, 3), (3, 3), (6, 3), (9, 2), (11, 1))
+SPLIT = ((0, 3), (3, 3), (6, 2), (8, 2), (10, 1))
 CHUNKS = len(SPLIT)
-ZF, ZN = 12, 3
+ZF, ZN = 11, 4
 PITCH = 40
 OPITCH = 24
 
@@ -133,9 +133,16 @@
     ahead = chip(lax.rem(x + 1, NX), z, lax.rem(y + 1, NY))
     behind = chip(lax.rem(x + NX - 1, NX), z, lax.rem(y + NY - 1, NY))
     z_near = [chip(x, lax.rem(z + n, NZ), y) for n in (1, NZ - 1, 2, NZ - 2)]
-    for h in range(2):
-        greet(up, h)
-        greet(down, h)
+    corner = (z == 0) & (y == 0)
+    relaying = (z == 0) & (y == NY - 1)
+
+    @pl.when(jnp.logical_not((z == NZ - 1) & (y == NY - 1)))
+    def _():
+        greet(up, 0)
+        greet(up, 1)
+
+    greet(down, 0)
+    greet(down, 1)
     for dom in z_near:
         greet(dom, 0)
         greet(dom, 1)
@@ -195,7 +202,7 @@
             metas[n] = table[n : n + 1]
     ocean_in.wait()
 
-    pl.semaphore_wait(barrier, 4 + 8 + 3 + 6 + 2 + 1)
+    pl.semaphore_wait(barrier, jnp.where(corner, 2, 4) + 8 + 3 + 6 + 2 + 1)
 
     def remote(src, dst, send, recv, dom, core):
         return pltpu.make_async_remote_copy(
@@ -230,8 +237,6 @@
         remote(relay, half.at[:, right], oc_send.at[6 + n], oc_recv.at[2 + n], below, h)
         for n, h in enumerate((c, other))
     ]
-    corner = (z == 0) & (y == 0)
-    relaying = (z == 0) & (y == NY - 1)
     for copy in upward:
         copy.start()
 
@@ -307,38 +312,6 @@
         return 0
 
     pl.semaphore_wait(near_sem, 5)
-
-    remote(sent_meta.at[15], got_meta.at[30], me_send, me_recv, d, other).start()
-    remote(zsent_meta.at[7], zraw_meta.at[14], zm_send, zm_recv, d, other).start()
-
-    def send_meta(j, _):
-        for h in range(2):
-            remote(
-                sent_meta.at[j - 1],
-                got_meta.at[(j - 1) * 2 + c],
-                me_send,
-                me_recv,
-                plane_chip(j),
-                h,
-            ).start()
-        return 0
-
-    def send_zmeta(dz, _):
-        for h in range(2):
-            remote(
-                zsent_meta.at[dz - 1],
-                zraw_meta.at[(dz - 1) * 2 + c],
-                zm_send,
-                zm_recv,
-                line_chip(dz),
-                h,
-            ).start()
-        return 0
-
-    lax.fori_loop(1, PLANE, send_meta, 0)
-    lax.fori_loop(1, NZ, send_zmeta, 0)
-    got_meta[31] = sent_meta[15]
-    zraw_meta[15] = zsent_meta[7]
 
     def z_rows(start):
         return pl.ds(pl.multiple_of(start * 32, 32), 32)
@@ -391,6 +364,38 @@
         ]
 
     send_plane(0)
+    remote(sent_meta.at[15], got_meta.at[30], me_send, me_recv, d, other).start()
+    remote(zsent_meta.at[7], zraw_meta.at[14], zm_send, zm_recv, d, other).start()
+
+    def send_meta(j, _):
+        for h in range(2):
+            remote(
+                sent_meta.at[j - 1],
+                got_meta.at[(j - 1) * 2 + c],
+                me_send,
+                me_recv,
+                plane_chip(j),
+                h,
+            ).start()
+        return 0
+
+    def send_zmeta(dz, _):
+        for h in range(2):
+            remote(
+                zsent_meta.at[dz - 1],
+                zraw_meta.at[(dz - 1) * 2 + c],
+                zm_send,
+                zm_recv,
+                line_chip(dz),
+                h,
+            ).start()
+        return 0
+
+    lax.fori_loop(1, PLANE, send_meta, 0)
+    lax.fori_loop(1, NZ, send_zmeta, 0)
+    got_meta[31] = sent_meta[15]
+    zraw_meta[15] = zsent_meta[7]
+
     for g in range(ZF, ZF + ZN):
         turn(g, 0)
     for h in range(2):

time: 47.6 us -> 42.6 us (0.89)
  Pallas kernels: 46.9 us -> 41.9 us
    pallas_call x1, Pallas kernels: 46.9 us -> 41.9 us  [local(): pl.pallas_call(kernel, out_shape=jax.ShapeDtypeStruct((HALF, NB * BLK), f...]
where the time goes in v5:
time: 42.6 us; the launch traced here: 42.5 us
  Pallas kernels  41.9 us (98%)
  local copies, waits for them, and re-layouts  0.66 us (2%)
    pallas_call x1, Pallas kernels, local(): pl.pallas_call(kernel, out_shape=jax.ShapeDtypeStruct((HALF, NB * BLK), f...  41.9 us

profile of v5, /device:TPU:1, one launch (start us, length us, event | category | flops | bytes accessed | tf_op | source)
XLA Modules:
  0.0 42.5 jit_solution(2771300515031851507)
XLA Ops:
  0.0 41.9 %shard_map.73 = f32[15,2048]{1,0:T(8,128)S(1)} custom-call(bf16[15,2048]{1,0:T(8,128)(2,1)} %ocean_hbm.1, bf16[16,512,256]{2,1,0:T(8,128)(2,1)} %bitcast.5, s32[4,16]{1,0:T(4,128)} %bitcast.7, bf16[64,384,128]{2,1,0:T(8,128)(2,1)} %rw_hbm.1, s32[1,64]{1,0:T(1,128)} %bitcast.8, s32[1,64]{1,0:T(1,128)} %bitcast.9, s32[16,128]{1,0:T(8,128)} %bitcast.6), custom_call_target="tpu_custom_call" | custom-call | tf_op jit(solution)/shard_map/pallas_call | solution.py:554
  41.9 0.7 %copy.9 = f32[15,2048]{1,0:T(8,128)} copy(f32[15,2048]{1,0:T(8,128)S(1)} %shard_map.73) | data formatting | bytes 245760

commit v6 on v5

--- a/solution.py
+++ b/solution.py
@@ -18,9 +18,12 @@
 TILES = 64
 SLOTS = 16
 SRC_ROWS = 16
-SPLIT = ((0, 3), (3, 3), (6, 2), (8, 2), (10, 1))
+SPLIT = ((0, 4), (4, 4), (8, 2), (10, 1))
 CHUNKS = len(SPLIT)
 ZF, ZN = 11, 4
+SENDS = (0, "meta", (0, 4), 1, 2, 3)
+WAITS = (0, 1, "z", 2, 3)
+Z_ORDER = (4, 3, 5, 2, 6, 1, 7)
 PITCH = 40
 OPITCH = 24
 
@@ -79,6 +82,7 @@
     oc_send,
     oc_recv,
     near_sem,
+    late_sem,
     me_send,
     me_recv,
     pl_send,
@@ -132,7 +136,6 @@
     y_ring = [chip(x, z, lax.rem(y + n, NY)) for n in range(1, NY)]
     ahead = chip(lax.rem(x + 1, NX), z, lax.rem(y + 1, NY))
     behind = chip(lax.rem(x + NX - 1, NX), z, lax.rem(y + NY - 1, NY))
-    z_near = [chip(x, lax.rem(z + n, NZ), y) for n in (1, NZ - 1, 2, NZ - 2)]
     corner = (z == 0) & (y == 0)
     relaying = (z == 0) & (y == NY - 1)
 
@@ -143,16 +146,27 @@
 
     greet(down, 0)
     greet(down, 1)
-    for dom in z_near:
-        greet(dom, 0)
-        greet(dom, 1)
+    for n in (1, 2):
+        above, under = line_chip(n), line_chip(NZ - n)
+        for h in range(2):
+            greet(under, h)
+
+        @pl.when(z < NZ - n)
+        def _(above=above):
+            greet(above, 0)
+            greet(above, 1)
+
     for dom in y_ring:
         greet(dom, c)
     for n in range(1, NX):
         for h in range(2):
             greet(chip(lax.rem(x + n, NX), z, y), h)
-    greet(ahead, c)
-    greet(behind, c)
+
+    @pl.when(z == 0)
+    def _():
+        greet(ahead, c)
+        greet(behind, c)
+
     greet(d, other)
 
     small[0].wait()
@@ -202,7 +216,9 @@
             metas[n] = table[n : n + 1]
     ocean_in.wait()
 
-    pl.semaphore_wait(barrier, jnp.where(corner, 2, 4) + 8 + 3 + 6 + 2 + 1)
+    greeted = 4 + 4 + 3 + 6 + 1 + jnp.where(z >= 1, 2, 0) + jnp.where(z >= 2, 2, 0)
+    greeted = greeted + jnp.where(z == 0, 2, 0) - jnp.where(corner, 2, 0)
+    pl.semaphore_wait(barrier, greeted)
 
     def remote(src, dst, send, recv, dom, core):
         return pltpu.make_async_remote_copy(
@@ -250,8 +266,21 @@
             copy.start()
 
     sideways.start()
-    for dom in y_ring + z_near[2:]:
+    for dom in y_ring:
         greet(dom, c, near_sem)
+    for n in (1, 2):
+
+        @pl.when(z >= NZ - n)
+        def _(n=n):
+            greet(line_chip(n), 0, late_sem)
+            greet(line_chip(n), 1, late_sem)
+
+    @pl.when(z < 2)
+    def _():
+        pl.semaphore_wait(late_sem, jnp.where(z == 0, 4, 2))
+
+    greet(line_chip(2), c, near_sem)
+    greet(line_chip(NZ - 2), c, near_sem)
     @pl.when(relaying)
     def _():
         to_relay.wait_recv()
@@ -363,69 +392,77 @@
             pl.ds(c * HALF + f0, fn), own_rows, :
         ]
 
-    send_plane(0)
-    remote(sent_meta.at[15], got_meta.at[30], me_send, me_recv, d, other).start()
-    remote(zsent_meta.at[7], zraw_meta.at[14], zm_send, zm_recv, d, other).start()
-
-    def send_meta(j, _):
+    def send_metas():
+        remote(sent_meta.at[15], got_meta.at[30], me_send, me_recv, d, other).start()
+        remote(zsent_meta.at[7], zraw_meta.at[14], zm_send, zm_recv, d, other).start()
+
+        def send_meta(j, _):
+            for h in range(2):
+                remote(
+                    sent_meta.at[j - 1],
+                    got_meta.at[(j - 1) * 2 + c],
+                    me_send,
+                    me_recv,
+                    plane_chip(j),
+                    h,
+                ).start()
+            return 0
+
+        def send_zmeta(dz, _):
+            for h in range(2):
+                remote(
+                    zsent_meta.at[dz - 1],
+                    zraw_meta.at[(dz - 1) * 2 + c],
+                    zm_send,
+                    zm_recv,
+                    line_chip(dz),
+                    h,
+                ).start()
+            return 0
+
+        lax.fori_loop(1, PLANE, send_meta, 0)
+        lax.fori_loop(1, NZ, send_zmeta, 0)
+        got_meta[31] = sent_meta[15]
+        zraw_meta[15] = zsent_meta[7]
+
+    def send_z_first(g0, gn):
+        for g in range(g0, g0 + gn):
+            turn(ZF + g, 0)
         for h in range(2):
-            remote(
-                sent_meta.at[j - 1],
-                got_meta.at[(j - 1) * 2 + c],
-                me_send,
-                me_recv,
-                plane_chip(j),
-                h,
-            ).start()
-        return 0
-
-    def send_zmeta(dz, _):
-        for h in range(2):
-            remote(
-                zsent_meta.at[dz - 1],
-                zraw_meta.at[(dz - 1) * 2 + c],
-                zm_send,
-                zm_recv,
-                line_chip(dz),
-                h,
-            ).start()
-        return 0
-
-    lax.fori_loop(1, PLANE, send_meta, 0)
-    lax.fori_loop(1, NZ, send_zmeta, 0)
-    got_meta[31] = sent_meta[15]
-    zraw_meta[15] = zsent_meta[7]
-
-    for g in range(ZF, ZF + ZN):
-        turn(g, 0)
-    for h in range(2):
-        for g in range(ZN):
-            zsent[h * ZN + g] = dot(zpack[...], fields[h * HALF + ZF + g]).astype(bf16)
-    remote(
-        zsent.at[pl.ds(other * ZN, ZN), z_rows(7)],
-        zraw.at[:, z_rows(14)],
-        zr_send,
-        zr_recv,
-        d,
-        other,
-    ).start()
-
-    def send_raw(dz, _):
-        for h in range(2):
-            remote(
-                zsent.at[pl.ds(h * ZN, ZN), z_rows(dz - 1)],
-                zraw.at[:, z_rows((dz - 1) * 2 + c)],
-                zr_send,
-                zr_recv,
-                line_chip(dz),
-                h,
-            ).start()
-        return 0
-
-    lax.fori_loop(1, NZ, send_raw, 0)
-    zraw[:, z_rows(15), :] = zsent[pl.ds(c * ZN, ZN), z_rows(7), :]
-    for k in range(1, CHUNKS):
-        send_plane(k)
+            for g in range(g0, g0 + gn):
+                zsent[h * ZN + g] = dot(zpack[...], fields[h * HALF + ZF + g]).astype(bf16)
+        remote(
+            zsent.at[pl.ds(other * ZN + g0, gn), z_rows(7)],
+            zraw.at[pl.ds(g0, gn), z_rows(14)],
+            zr_send,
+            zr_recv,
+            d,
+            other,
+        ).start()
+
+        def send_raw(dz, _):
+            for h in range(2):
+                remote(
+                    zsent.at[pl.ds(h * ZN + g0, gn), pl.ds((dz - 1) * 32, 32)],
+                    zraw.at[pl.ds(g0, gn), z_rows((dz - 1) * 2 + c)],
+                    zr_send,
+                    zr_recv,
+                    line_chip(dz),
+                    h,
+                ).start()
+            return 0
+
+        for dz in Z_ORDER:
+            send_raw(dz, 0)
+        zraw[pl.ds(g0, gn), z_rows(15), :] = zsent[pl.ds(c * ZN + g0, gn), z_rows(7), :]
+
+    for step in SENDS:
+        if step == "meta":
+            send_metas()
+        elif isinstance(step, tuple):
+            send_z_first(*step)
+        else:
+            send_plane(step)
 
     most, z_most = got_meta.at[pl.ds(0, 31)], zraw_meta.at[pl.ds(0, 15)]
     pltpu.make_async_copy(most, most, me_recv).wait()
@@ -461,8 +498,8 @@
 
         def send_z(dz, _):
             remote(
-                part.at[chunk, pl.ds(pl.multiple_of(dz * SLOTS, SLOTS), SLOTS)],
-                zgot.at[chunk, pl.ds(pl.multiple_of((dz - 1) * SLOTS, SLOTS), SLOTS)],
+                part.at[chunk, pl.ds(dz * SLOTS, SLOTS)],
+                zgot.at[chunk, pl.ds((dz - 1) * SLOTS, SLOTS)],
                 z_send.at[k],
                 z_recv.at[k],
                 line_chip(dz),
@@ -470,28 +507,30 @@
             ).start()
             return 0
 
-        lax.fori_loop(1, NZ, send_z, 0)
-
-    for k in range(CHUNKS - 2):
-        from_plane(k)
-
-    pltpu.make_async_copy(zraw.at[:, z_but_own], zraw.at[:, z_but_own], zr_recv).wait()
-    for g in range(ZN):
-        total = dot(zselect[...], zraw[g])
-        zown[g] = total[15 * SLOTS :]
-        zpart[g] = total.astype(bf16)
-
-    def send_sums(j, _):
-        rows = pl.ds(pl.multiple_of((j - 1) * SLOTS, SLOTS), SLOTS)
-        remote(
-            zpart.at[:, rows], zlast.at[:, rows], zp_send, zp_recv, plane_chip(j), c
-        ).start()
-        return 0
-
-    lax.fori_loop(1, PLANE, send_sums, 0)
-
-    for k in range(CHUNKS - 2, CHUNKS):
-        from_plane(k)
+        for dz in Z_ORDER:
+            send_z(dz, 0)
+
+    def from_z_first():
+        pltpu.make_async_copy(zraw.at[:, z_but_own], zraw.at[:, z_but_own], zr_recv).wait()
+        for g in range(ZN):
+            total = dot(zselect[...], zraw[g])
+            zown[g] = total[15 * SLOTS :]
+            zpart[g] = total.astype(bf16)
+
+        def send_sums(j, _):
+            rows = pl.ds(pl.multiple_of((j - 1) * SLOTS, SLOTS), SLOTS)
+            remote(
+                zpart.at[:, rows], zlast.at[:, rows], zp_send, zp_recv, plane_chip(j), c
+            ).start()
+            return 0
+
+        lax.fori_loop(1, PLANE, send_sums, 0)
+
+    for step in WAITS:
+        if step == "z":
+            from_z_first()
+        else:
+            from_plane(step)
 
     def from_line(k):
         f0, fn = SPLIT[k]
@@ -593,6 +632,7 @@
             dma((8,)),
             dma((6,)),
             pltpu.SemaphoreType.REGULAR,
+            pltpu.SemaphoreType.REGULAR,
             dma,
             dma,
             dma((CHUNKS,)),

time: 42.6 us -> 41.6 us (0.977)
  Pallas kernels: 41.9 us -> 40.9 us
    pallas_call x1, Pallas kernels: 41.9 us -> 40.9 us  [local(): pl.pallas_call(kernel, out_shape=jax.ShapeDtypeStruct((HALF, NB * BLK), f...]
where the time goes in v6:
time: 41.6 us
  Pallas kernels  40.9 us (98%)
  local copies, waits for them, and re-layouts  0.66 us (2%)
    pallas_call x1, Pallas kernels, local(): pl.pallas_call(kernel, out_shape=jax.ShapeDtypeStruct((HALF, NB * BLK), f...  40.9 us

profile of v6, /device:TPU:1, one launch (start us, length us, event | category | flops | bytes accessed | tf_op | source)
XLA Modules:
  0.0 41.6 jit_solution(7347353815212896251)
XLA Ops:
  0.0 40.9 %shard_map.73 = f32[15,2048]{1,0:T(8,128)S(1)} custom-call(bf16[15,2048]{1,0:T(8,128)(2,1)} %ocean_hbm.1, bf16[16,512,256]{2,1,0:T(8,128)(2,1)} %bitcast.5, s32[4,16]{1,0:T(4,128)} %bitcast.7, bf16[64,384,128]{2,1,0:T(8,128)(2,1)} %rw_hbm.1, s32[1,64]{1,0:T(1,128)} %bitcast.8, s32[1,64]{1,0:T(1,128)} %bitcast.9, s32[16,128]{1,0:T(8,128)} %bitcast.6), custom_call_target="tpu_custom_call" | custom-call | tf_op jit(solution)/shard_map/pallas_call | solution.py:593
  40.9 0.7 %copy.9 = f32[15,2048]{1,0:T(8,128)} copy(f32[15,2048]{1,0:T(8,128)S(1)} %shard_map.73) | data formatting | bytes 245760

commit v7 on v6

--- a/solution.py
+++ b/solution.py
@@ -306,7 +306,7 @@
         cont[pl.ds(pl.multiple_of(t * PITCH, 8), 32), :] = dot(wide[s + NH], rw[t, 0:BLK, :])
         return 0
 
-    lax.fori_loop(0, TILES, remap_values, 0, unroll=8)
+    lax.fori_loop(0, TILES, remap_values, 0, unroll=16)
     for copy in upward + downward:
         copy.wait_recv()
     spread_blocks((0, 1, NH + NB, NH + NB + 1))
@@ -324,14 +324,14 @@
         )
         return 0
 
-    lax.fori_loop(0, NB, gradient, 0, unroll=4)
+    lax.fori_loop(0, NB, gradient, 0, unroll=16)
     def remap(t, _):
         s = jnp.maximum(src_ref[0, t] - own_block, 0)
         at = pl.ds(pl.multiple_of(t * PITCH, 8), 32)
         cont[at, :] = cont[at, :] + dot(grads[s], rw[t, BLK:, :])
         return 0
 
-    lax.fori_loop(0, TILES, remap, 0, unroll=8)
+    lax.fori_loop(0, TILES, remap, 0, unroll=32)
 
     def turn(g, _):
         for h in range(2):

time: 41.6 us -> 40.5 us (0.974)
  Pallas kernels: 40.9 us -> 39.8 us
    pallas_call x1, Pallas kernels: 40.9 us -> 39.8 us  [local(): pl.pallas_call(kernel, out_shape=jax.ShapeDtypeStruct((HALF, NB * BLK), f...]
where the time goes in v7:
time: 40.5 us; the launch traced here: 40.4 us
  Pallas kernels  39.8 us (98%)
  local copies, waits for them, and re-layouts  0.66 us (2%)
    pallas_call x1, Pallas kernels, local(): pl.pallas_call(kernel, out_shape=jax.ShapeDtypeStruct((HALF, NB * BLK), f...  39.8 us

profile of v7, /device:TPU:1, one launch (start us, length us, event | category | flops | bytes accessed | tf_op | source)
XLA Modules:
  0.0 40.4 jit_solution(11430534762420058368)
XLA Ops:
  0.0 39.8 %shard_map.73 = f32[15,2048]{1,0:T(8,128)S(1)} custom-call(bf16[15,2048]{1,0:T(8,128)(2,1)} %ocean_hbm.1, bf16[16,512,256]{2,1,0:T(8,128)(2,1)} %bitcast.5, s32[4,16]{1,0:T(4,128)} %bitcast.7, bf16[64,384,128]{2,1,0:T(8,128)(2,1)} %rw_hbm.1, s32[1,64]{1,0:T(1,128)} %bitcast.8, s32[1,64]{1,0:T(1,128)} %bitcast.9, s32[16,128]{1,0:T(8,128)} %bitcast.6), custom_call_target="tpu_custom_call" | custom-call | tf_op jit(solution)/shard_map/pallas_call | solution.py:593
  39.8 0.7 %copy.9 = f32[15,2048]{1,0:T(8,128)} copy(f32[15,2048]{1,0:T(8,128)S(1)} %shard_map.73) | data formatting | bytes 245760

commit v8 on v7

--- a/solution.py
+++ b/solution.py
@@ -355,9 +355,12 @@
         for g in range(f0, f0 + fn):
             turn(g, 0)
         for h in range(2):
-            for g in range(f0, f0 + fn):
-                f = h * HALF + g
-                sent[f] = dot(pack[...], fields[f]).astype(bf16)
+            for g in range(f0, f0 + fn, 2):
+                f, n = h * HALF + g, min(2, f0 + fn - g)
+                pair = jnp.concatenate([fields[f + i] for i in range(n)], axis=1)
+                packed = dot(pack[...], pair).astype(bf16)
+                for i in range(n):
+                    sent[f + i] = packed[:, i * BLK : (i + 1) * BLK]
         chunk = pl.ds(f0, fn)
         remote(
             sent.at[pl.ds(other * HALF + f0, fn), own_rows],
@@ -491,10 +494,14 @@
         chunk = pl.ds(f0, fn)
         arrived = got.at[chunk, all_but_own]
         pltpu.make_async_copy(arrived, arrived, pl_recv.at[k]).wait()
-        for g in range(f0, f0 + fn):
-            total = dot(select[...], got[g])
-            own[g] = total[0:SLOTS]
-            part[g] = total.astype(bf16)
+        for g in range(f0, f0 + fn, 2):
+            n = min(2, f0 + fn - g)
+            pair = jnp.concatenate([got[g + i] for i in range(n)], axis=1)
+            totals = dot(select[...], pair)
+            for i in range(n):
+                total = totals[:, i * BLK : (i + 1) * BLK]
+                own[g + i] = total[0:SLOTS]
+                part[g + i] = total.astype(bf16)
 
         def send_z(dz, _):
             remote(

time: 40.5 us -> 40.6 us (level)
  no operation moved by 1% of the time
where the time goes in v8:
time: 40.6 us
  Pallas kernels  39.9 us (98%)
  local copies, waits for them, and re-layouts  0.66 us (2%)
    pallas_call x1, Pallas kernels, local(): pl.pallas_call(kernel, out_shape=jax.ShapeDtypeStruct((HALF, NB * BLK), f...  39.9 us

profile of v8, /device:TPU:1, one launch (start us, length us, event | category | flops | bytes accessed | tf_op | source)
XLA Modules:
  0.0 40.6 jit_solution(9717475068758479484)
XLA Ops:
  0.0 39.9 %shard_map.73 = f32[15,2048]{1,0:T(8,128)S(1)} custom-call(bf16[15,2048]{1,0:T(8,128)(2,1)} %ocean_hbm.1, bf16[16,512,256]{2,1,0:T(8,128)(2,1)} %bitcast.5, s32[4,16]{1,0:T(4,128)} %bitcast.7, bf16[64,384,128]{2,1,0:T(8,128)(2,1)} %rw_hbm.1, s32[1,64]{1,0:T(1,128)} %bitcast.8, s32[1,64]{1,0:T(1,128)} %bitcast.9, s32[16,128]{1,0:T(8,128)} %bitcast.6), custom_call_target="tpu_custom_call" | custom-call | tf_op jit(solution)/shard_map/pallas_call | solution.py:600
  39.9 0.7 %copy.9 = f32[15,2048]{1,0:T(8,128)} copy(f32[15,2048]{1,0:T(8,128)S(1)} %shard_map.73) | data formatting | bytes 245760
